TPU v7x, 512 devices: a whole 4x8x8 slice. The times are simulated.
512 devices in a mesh: wide: 64 (over z_hi, y, core), narrow: 8 (over z_lo, x).
Axes of the slice: x: 4, y: 8, z: 8 (z_hi: 4, z_lo: 2; z = z_hi * 2 + z_lo), core: 2. Of those that a mesh axis runs over, the one named last changes fastest.
Arguments:
- concentrations: float32 [256, 512, 256], P('wide', 'narrow'), may hold values from 0.1 to 2
- wind_speeds: bfloat16 [2, 2, 512, 256], P(None, None, ('narrow', 'wide')), may hold values from -0.59765625 to 0.59765625
- rate_constants: float32 [768], replicated, may hold values from 0.05 to 1
- reactants: int32 [768, 2], replicated, may hold values from 0 to 255
- products: int32 [768, 2], replicated, may hold values from 0 to 255
Outputs:
- after_chemistry: float32 [256, 512, 256], P(None, ('narrow', 'wide'))
Inputs may be any that keep to these rules, and one draw needn't show every extreme that they name: `reactants`: each entry is a species number. `products`: each entry is a species number.
All inputs are finite; a program needn't handle non-finite values.
Results may differ from a plain program's by a relative error of at most 0.0003.
Values may be sent and summed in bfloat16 or wider, within the bound.
No kernel may reach another device: no remote copies, remote signals or barrier semaphores. Data moves between devices by JAX's collectives and lax.ppermute only.
A program may use at most 64 MiB of HBM per device.

v0:
```python
import jax
import jax.numpy as jnp
from jax import lax
from jax.sharding import PartitionSpec as P

S = 256
SUB = 2
SECTIONS = 6


DIFFUSION = 0.1
CHEM_STEP = 0.02


def laid_out(tiles, dim):
    shape = list(tiles.shape[1:])
    shape[dim] *= tiles.shape[0]
    return jnp.moveaxis(tiles, 0, dim).reshape(shape)


def sent_to_all(shard, axis):
    peers = lax.axis_size(axis)
    return lax.all_to_all(
        jnp.broadcast_to(shard[None], (peers, *shard.shape)), axis, 0, 0, tiled=True
    )


def gather_directly(shard, axis, dim):
    return laid_out(sent_to_all(shard, axis), dim)


def padded(cells, sides, width):
    for axis, dim in sides:
        count = lax.axis_size(axis)
        head = lax.slice_in_dim(cells, 0, width, axis=dim)
        tail = lax.slice_in_dim(cells, cells.shape[dim] - width, cells.shape[dim], axis=dim)
        cells = jnp.concatenate(
            [
                lax.ppermute(tail, axis, [(i, (i + 1) % count) for i in range(count)]),
                cells,
                lax.ppermute(head, axis, [((i + 1) % count, i) for i in range(count)]),
            ],
            axis=dim,
        )
    return cells


def take_range(array, begin_at, end_at, along):
    along = along % array.ndim
    index = [slice(None)] * array.ndim
    index[along] = slice(begin_at, end_at)
    return array[tuple(index)]


def minmod(first_jump, second_jump):
    return jnp.maximum(0.0, jnp.minimum(first_jump, second_jump)) + jnp.minimum(
        0.0, jnp.maximum(first_jump, second_jump)
    )


def sweep_axis(extended, speeds, along, closed):
    length = extended.shape[along]
    speed_face = 0.5 * (
        take_range(speeds, 0, length - 1, along) + take_range(speeds, 1, length, along)
    )
    jumps = take_range(extended, 1, length, along) - take_range(extended, 0, length - 1, along)
    slopes = minmod(
        take_range(jumps, 0, length - 2, along), take_range(jumps, 1, length - 1, along)
    )
    inner_speed = take_range(speed_face, 1, length - 2, along)
    left_value = take_range(extended, 1, length - 2, along) + 0.5 * (
        1.0 - inner_speed
    ) * take_range(slopes, 0, length - 3, along)
    right_value = take_range(extended, 2, length - 1, along) - 0.5 * (
        1.0 + inner_speed
    ) * take_range(slopes, 1, length - 2, along)
    face_flux = inner_speed * jnp.where(
        inner_speed >= 0.0, left_value, right_value
    ) - DIFFUSION * take_range(jumps, 1, length - 2, along)
    if closed:
        position = lax.broadcasted_iota(jnp.int32, face_flux.shape, along % face_flux.ndim)
        face_flux = jnp.where((position > 0) & (position < length - 4), face_flux, 0.0)
    return take_range(extended, 2, length - 2, along) - (
        take_range(face_flux, 1, length - 3, along) - take_range(face_flux, 0, length - 4, along)
    )


def sweep_second(tracer, speeds):
    pad_tracer = [(0, 0)] * (tracer.ndim - 1) + [(2, 2)]
    pad_speeds = [(0, 0)] * (speeds.ndim - 1) + [(2, 2)]
    return sweep_axis(
        jnp.pad(tracer, pad_tracer, mode="edge"), jnp.pad(speeds, pad_speeds, mode="edge"), -1, True
    )


def react_cells(cell_block, rate_constants, first_ids, second_ids, net_matrix):
    for section_index in range(SECTIONS):
        rate_values = (
            rate_constants[:, None]
            * jnp.take(cell_block, first_ids, axis=0)
            * jnp.take(cell_block, second_ids, axis=0)
        )
        cell_block = cell_block + CHEM_STEP * jnp.dot(
            net_matrix, rate_values, precision=lax.Precision.HIGHEST
        )
    return cell_block


def on_device(concentrations, wind_speeds, rate_constants, reactants, products):
    groups = concentrations.shape[0]
    row_count = wind_speeds.shape[2]
    columns = wind_speeds.shape[3]
    wide_count = lax.axis_size("wide")
    planes = wind_speeds.reshape(SUB * 2, row_count, columns)
    gathered = gather_directly(planes, "wide", 1).astype(jnp.float32)
    tracer = concentrations
    stacked = jnp.concatenate([tracer, gathered], 0)
    extended = padded(stacked, (("narrow", 1),), 4)
    wind_rims = extended[groups:]
    tracer = sweep_axis(extended[:groups], wind_rims[0], -2, False)
    tracer = sweep_second(tracer, wind_rims[1, 2:-2])
    tracer = sweep_axis(tracer, wind_rims[2, 2:-2], -2, False)
    tracer = sweep_second(tracer, wind_rims[3, 4:-4])
    species_ids = lax.broadcasted_iota(jnp.int32, (S, rate_constants.shape[0]), 0)

    def one_hot(species_column):
        return (species_ids == species_column[None, :]).astype(jnp.float32)

    net_matrix = (
        one_hot(products[:, 0])
        + one_hot(products[:, 1])
        - one_hot(reactants[:, 0])
        - one_hot(reactants[:, 1])
    )
    first_ids = reactants[:, 0]
    second_ids = reactants[:, 1]
    shaped = tracer.reshape(groups, wide_count, row_count, columns)
    cell_block = lax.all_to_all(shaped, "wide", split_axis=1, concat_axis=0, tiled=True)
    flattened = cell_block.reshape(cell_block.shape[0], -1)
    regrouped = react_cells(flattened, rate_constants, first_ids, second_ids, net_matrix).reshape(
        cell_block.shape
    )
    return regrouped.reshape(S, row_count, columns)


def solution(mesh):
    return jax.shard_map(
        on_device,
        mesh=mesh,
        in_specs=(
            P("wide", "narrow", None),
            P(None, None, ("narrow", "wide"), None),
            P(),
            P(),
            P(),
        ),
        out_specs=P(None, ("narrow", "wide"), None),
        check_vma=False,
    )
```

profile of v0, /device:TPU:1, one launch (start us, length us, event | category | flops | bytes accessed | tf_op | source)
XLA Modules:
  0.0 104.8 jit_solution(10963624818956089854)
XLA Ops:
  0.0 0.7 broadcast_in_dim.53
  0.7 0.7 broadcast_in_dim.54
  1.4 17.7 %all-to-all-start = ((bf16[64,4,1,256]{3,1,2,0:T(4,128)(2,1)}), bf16[64,4,1,256]{3,1,2,0:T(4,128)(2,1)S(1)}, u32[]{:S(2)}, u32[]{:S(2)}) async-start(bf16[64,4,1,256]{3,1,2,0:T(4,128)(2,1)} %broadcast_in_dim.54), calls=%async_computation | async-start | bytes 262144 | tf_op jit(solution)/shard_map/all_to_all | solution.py:23
  19.2 0.2 copy.10
  19.4 12.5 %all-to-all-done = bf16[64,4,1,256]{3,1,2,0:T(4,128)(2,1)S(1)} async-done(((bf16[64,4,1,256]{3,1,2,0:T(4,128)(2,1)}), bf16[64,4,1,256]{3,1,2,0:T(4,128)(2,1)S(1)}, u32[]{:S(2)}, u32[]{:S(2)}) %all-to-all-start) | async-done | bytes 131104 | tf_op jit(solution)/shard_map/all_to_all | solution.py:23
  32.1 0.2 slice_reduce_fusion.3
  32.3 3.1 %collective-permute-start = (f32[8,4,256]{2,0,1:T(8,128)S(1)}, f32[8,4,256]{2,0,1:T(8,128)S(1)}, u32[]{:S(2)}, u32[]{:S(2)}) collective-permute-start(f32[8,4,256]{2,0,1:T(8,128)S(1)} %get-tuple-element.22), channel_id=1, source_target_pairs={{0,1},{1,2},{2,3},{3,4},{4,5},{5,6},{6,7},{7,0},{8,9},{9,10},{10,1... | collective-permute-start | bytes 98312 | tf_op jit(solution)/shard_map/ppermute | solution.py:39
  35.4 4.3 %collective-permute-start.1 = (f32[8,4,256]{2,0,1:T(8,128)S(1)}, f32[8,4,256]{2,0,1:T(8,128)S(1)}, u32[]{:S(2)}, u32[]{:S(2)}) collective-permute-start(f32[8,4,256]{2,0,1:T(8,128)S(1)} %get-tuple-element.23), channel_id=1, source_target_pairs={{1,0},{2,1},{3,2},{4,3},{5,4},{6,5},{7,6},{0,7},{9,8},{10,9},{11,1... | collective-permute-start | bytes 98312 | tf_op jit(solution)/shard_map/ppermute | solution.py:41
  39.8 0.1 pad_maximum_fusion.8
  40.0 0.1 broadcast_compare_fusion.1
  40.2 0.5 collective-permute-done.1
  40.7 0.1 pad_maximum_fusion
  41.4 0.2 slice_reduce_fusion.1
  41.8 0.1 pad_maximum_fusion.7
  42.0 0.1 broadcast_compare_fusion
  42.3 0.3 fusion.67
  42.6 0.1 fusion.97
  42.8 0.1 copy.11
  42.9 0.1 copy.13
  43.0 0.1 copy.14
  43.1 0.1 copy.12
  43.2 0.1 reshape.90
  43.4 0.1 reshape.91
  43.5 0.4 pad_maximum_fusion.3
  43.9 0.3 slice_subtract_fusion
  44.1 0.3 minimum_add_fusion
  44.4 0.8 fusion.8
  45.3 0.2 fusion.72
  45.7 0.3 fusion.74
  45.9 0.1 fusion.81
  46.0 0.1 fusion.98
  46.3 0.1 copy.17
  46.4 0.1 copy.18
  46.5 0.1 copy.16
  46.6 0.1 reshape.94
  46.7 0.1 reshape.95
  46.9 0.3 pad_maximum_fusion.6
  47.2 0.3 slice_subtract_fusion.1
  47.5 0.3 minimum_add_fusion.1
  47.8 0.8 fusion.14
  48.6 0.9 fusion.80
  49.5 5.6 %all-to-all-start.1 = ((f32[4,64,1,256]{3,0,2,1:T(4,128)}), f32[4,64,1,256]{3,0,2,1:T(4,128)S(1)}, u32[]{:S(2)}, u32[]{:S(2)}) async-start(f32[4,64,1,256]{3,0,2,1:T(4,128)} %fusion.80), calls=%async_computation.1 | async-start | bytes 524288 | tf_op jit(solution)/shard_map/all_to_all | solution.py:138
  55.1 0.7 copy-done.2
  55.9 13.3 %all-to-all-done.1 = f32[4,64,1,256]{3,0,2,1:T(4,128)S(1)} async-done(((f32[4,64,1,256]{3,0,2,1:T(4,128)}), f32[4,64,1,256]{3,0,2,1:T(4,128)S(1)}, u32[]{:S(2)}, u32[]{:S(2)}) %all-to-all-start.1) | async-done | bytes 262176 | tf_op jit(solution)/shard_map/all_to_all | solution.py:138
  69.3 2.1 %gather_fusion.1 = f32[768,256]{1,0:T(8,128)S(1)} fusion(f32[256,256]{1,0:T(8,128)S(1)} %reshape.97, s32[1024]{0:T(1024)S(1)} %pad_clamp_fusion), kind=kCustom, calls=%fused_computation.1.clone | custom fusion | bytes 1575936 | tf_op jit(solution)/shard_map/jit(_take)/gather | solution.py:101
  71.4 2.1 %gather_fusion = f32[768,256]{1,0:T(8,128)S(1)} fusion(f32[256,256]{1,0:T(8,128)S(1)} %reshape.97, s32[1024]{0:T(1024)S(1)} %pad_clamp_fusion.1), kind=kCustom, calls=%fused_computation.clone | custom fusion | bytes 1575936 | tf_op jit(solution)/shard_map/jit(_take)/gather | solution.py:100
  73.5 0.7 copy-done.3
  74.2 1.4 %fusion.5 = f32[256,256]{1,0:T(8,128)S(1)} fusion(f32[256,256]{1,0:T(8,128)S(1)} %reshape.97, f32[768,256]{1,0:T(8,128)S(1)} %gather_fusion.1, f32[768,256]{1,0:T(8,128)S(1)} %gather_fusion, f32[768]{0:T(1024)S(1)} %copy-done.3, s32[768]{0:T(1024)S(1)} %get-tuple-element.13, s32[768]{0:T(1024)S(1)} %get-tuple-element.12, s32[768]{0:T(1024)S(1)} %get-tuple-element.11, ...), kind=kOutput, calls=%fused_computation.23 | convolution fusion | flops 607059968 | bytes 2114048 | tf_op jit(solution)/shard_map/dot_general | solution.py:103
  75.6 2.1 %gather_fusion.3 = f32[768,256]{1,0:T(8,128)S(1)} fusion(f32[256,256]{1,0:T(8,128)S(1)} %fusion.5, s32[1024]{0:T(1024)S(1)} %pad_clamp_fusion), kind=kCustom, calls=%fused_computation.3.clone | custom fusion | bytes 1575936 | tf_op jit(solution)/shard_map/jit(_take)/gather | solution.py:101
  77.7 2.1 %gather_fusion.2 = f32[768,256]{1,0:T(8,128)S(1)} fusion(f32[256,256]{1,0:T(8,128)S(1)} %fusion.5, s32[1024]{0:T(1024)S(1)} %pad_clamp_fusion.1), kind=kCustom, calls=%fused_computation.2.clone | custom fusion | bytes 1575936 | tf_op jit(solution)/shard_map/jit(_take)/gather | solution.py:100
  79.8 1.4 %fusion.4 = f32[256,256]{1,0:T(8,128)S(1)} fusion(f32[256,256]{1,0:T(8,128)S(1)} %fusion.5, f32[768,256]{1,0:T(8,128)S(1)} %gather_fusion.3, f32[768,256]{1,0:T(8,128)S(1)} %gather_fusion.2, f32[768]{0:T(1024)S(1)} %copy-done.3, s32[768]{0:T(1024)S(1)} %get-tuple-element.13, s32[768]{0:T(1024)S(1)} %get-tuple-element.12, s32[768]{0:T(1024)S(1)} %get-tuple-element.11, ...), kind=kOutput, calls=%fused_computation.21 | convolution fusion | flops 607059968 | bytes 2114048 | tf_op jit(solution)/shard_map/dot_general | solution.py:103
  81.2 2.1 %gather_fusion.5 = f32[768,256]{1,0:T(8,128)S(1)} fusion(f32[256,256]{1,0:T(8,128)S(1)} %fusion.4, s32[1024]{0:T(1024)S(1)} %pad_clamp_fusion), kind=kCustom, calls=%fused_computation.5.clone | custom fusion | bytes 1575936 | tf_op jit(solution)/shard_map/jit(_take)/gather | solution.py:101
  83.3 2.1 %gather_fusion.4 = f32[768,256]{1,0:T(8,128)S(1)} fusion(f32[256,256]{1,0:T(8,128)S(1)} %fusion.4, s32[1024]{0:T(1024)S(1)} %pad_clamp_fusion.1), kind=kCustom, calls=%fused_computation.4.clone | custom fusion | bytes 1575936 | tf_op jit(solution)/shard_map/jit(_take)/gather | solution.py:100
  85.4 1.4 %fusion.3 = f32[256,256]{1,0:T(8,128)S(1)} fusion(f32[256,256]{1,0:T(8,128)S(1)} %fusion.4, f32[768,256]{1,0:T(8,128)S(1)} %gather_fusion.5, f32[768,256]{1,0:T(8,128)S(1)} %gather_fusion.4, f32[768]{0:T(1024)S(1)} %copy-done.3, s32[768]{0:T(1024)S(1)} %get-tuple-element.13, s32[768]{0:T(1024)S(1)} %get-tuple-element.12, s32[768]{0:T(1024)S(1)} %get-tuple-element.11, ...), kind=kOutput, calls=%fused_computation.19 | convolution fusion | flops 607059968 | bytes 2114048 | tf_op jit(solution)/shard_map/dot_general | solution.py:103
  86.8 2.1 %gather_fusion.7 = f32[768,256]{1,0:T(8,128)S(1)} fusion(f32[256,256]{1,0:T(8,128)S(1)} %fusion.3, s32[1024]{0:T(1024)S(1)} %pad_clamp_fusion), kind=kCustom, calls=%fused_computation.7.clone | custom fusion | bytes 1575936 | tf_op jit(solution)/shard_map/jit(_take)/gather | solution.py:101
  88.9 2.1 %gather_fusion.6 = f32[768,256]{1,0:T(8,128)S(1)} fusion(f32[256,256]{1,0:T(8,128)S(1)} %fusion.3, s32[1024]{0:T(1024)S(1)} %pad_clamp_fusion.1), kind=kCustom, calls=%fused_computation.6.clone | custom fusion | bytes 1575936 | tf_op jit(solution)/shard_map/jit(_take)/gather | solution.py:100
  91.0 1.4 %fusion.2 = f32[256,256]{1,0:T(8,128)S(1)} fusion(f32[256,256]{1,0:T(8,128)S(1)} %fusion.3, f32[768,256]{1,0:T(8,128)S(1)} %gather_fusion.7, f32[768,256]{1,0:T(8,128)S(1)} %gather_fusion.6, f32[768]{0:T(1024)S(1)} %copy-done.3, s32[768]{0:T(1024)S(1)} %get-tuple-element.13, s32[768]{0:T(1024)S(1)} %get-tuple-element.12, s32[768]{0:T(1024)S(1)} %get-tuple-element.11, ...), kind=kOutput, calls=%fused_computation.17 | convolution fusion | flops 607059968 | bytes 2114048 | tf_op jit(solution)/shard_map/dot_general | solution.py:103
  92.4 2.1 %gather_fusion.9 = f32[768,256]{1,0:T(8,128)S(1)} fusion(f32[256,256]{1,0:T(8,128)S(1)} %fusion.2, s32[1024]{0:T(1024)S(1)} %pad_clamp_fusion), kind=kCustom, calls=%fused_computation.9.clone | custom fusion | bytes 1575936 | tf_op jit(solution)/shard_map/jit(_take)/gather | solution.py:101
  94.5 2.3 %gather_fusion.8 = f32[768,256]{1,0:T(8,128)S(1)} fusion(f32[256,256]{1,0:T(8,128)S(1)} %fusion.2, s32[1024]{0:T(1024)S(1)} %pad_clamp_fusion.1), kind=kCustom, calls=%fused_computation.8.clone | custom fusion | bytes 1575936 | tf_op jit(solution)/shard_map/jit(_take)/gather | solution.py:100
  96.8 1.4 %fusion.1 = f32[256,256]{1,0:T(8,128)S(1)} fusion(f32[256,256]{1,0:T(8,128)S(1)} %fusion.2, f32[768,256]{1,0:T(8,128)S(1)} %gather_fusion.9, f32[768,256]{1,0:T(8,128)S(1)} %gather_fusion.8, f32[768]{0:T(1024)S(1)} %copy-done.3, s32[768]{0:T(1024)S(1)} %get-tuple-element.13, s32[768]{0:T(1024)S(1)} %get-tuple-element.12, s32[768]{0:T(1024)S(1)} %get-tuple-element.11, ...), kind=kOutput, calls=%fused_computation.15 | convolution fusion | flops 607059968 | bytes 2114048 | tf_op jit(solution)/shard_map/dot_general | solution.py:103
  98.2 2.1 %gather_fusion.11 = f32[768,256]{1,0:T(8,128)S(1)} fusion(f32[256,256]{1,0:T(8,128)S(1)} %fusion.1, s32[1024]{0:T(1024)S(1)} %pad_clamp_fusion), kind=kCustom, calls=%fused_computation.11.clone | custom fusion | bytes 1575936 | tf_op jit(solution)/shard_map/jit(_take)/gather | solution.py:101
  100.3 2.1 %gather_fusion.10 = f32[768,256]{1,0:T(8,128)S(1)} fusion(f32[256,256]{1,0:T(8,128)S(1)} %fusion.1, s32[1024]{0:T(1024)S(1)} %pad_clamp_fusion.1), kind=kCustom, calls=%fused_computation.10.clone | custom fusion | bytes 1575936 | tf_op jit(solution)/shard_map/jit(_take)/gather | solution.py:100
  102.5 1.4 %fusion.6 = f32[256,1,256]{2,0,1:T(8,128)S(1)} fusion(f32[256,256]{1,0:T(8,128)S(1)} %fusion.1, f32[768,256]{1,0:T(8,128)S(1)} %gather_fusion.11, f32[768,256]{1,0:T(8,128)S(1)} %gather_fusion.10, f32[768]{0:T(1024)S(1)} %copy-done.3, s32[768]{0:T(1024)S(1)} %get-tuple-element.13, s32[768]{0:T(1024)S(1)} %get-tuple-element.12, ...), kind=kOutput, calls=%fused_computation.24 | convolution fusion | flops 607059968 | bytes 2114048 | tf_op jit(solution)/shard_map/dot_general | solution.py:103
  103.8 1.0 copy.20
  (45 shorter events, 1.8 us)
Async XLA Ops:
  0.0 19.2 %copy-start = (f32[4,64,256]{2,1,0:T(8,128)S(1)}, f32[4,64,256]{2,1,0:T(8,128)}, u32[]{:S(2)}) copy-start(f32[4,64,256]{2,1,0:T(8,128)} %param.7) | copy-start | bytes 786436
  1.4 17.8 %copy-start.1 = (s32[768,2]{0,1:T(2,128)S(1)}, s32[768,2]{0,1:T(2,128)}, u32[]{:S(2)}) copy-start(s32[768,2]{0,1:T(2,128)} %param.10) | copy-start | bytes 18436
  1.4 30.5 %all-to-all-start = ((bf16[64,4,1,256]{3,1,2,0:T(4,128)(2,1)}), bf16[64,4,1,256]{3,1,2,0:T(4,128)(2,1)S(1)}, u32[]{:S(2)}, u32[]{:S(2)}) async-start(bf16[64,4,1,256]{3,1,2,0:T(4,128)(2,1)} %broadcast_in_dim.54), calls=%async_computation | async-start | bytes 262144 | tf_op jit(solution)/shard_map/all_to_all | solution.py:23
  32.3 7.9 %collective-permute-start = (f32[8,4,256]{2,0,1:T(8,128)S(1)}, f32[8,4,256]{2,0,1:T(8,128)S(1)}, u32[]{:S(2)}, u32[]{:S(2)}) collective-permute-start(f32[8,4,256]{2,0,1:T(8,128)S(1)} %get-tuple-element.22), channel_id=1, source_target_pairs={{0,1},{1,2},{2,3},{3,4},{4,5},{5,6},{6,7},{7,0},{8,9},{9,10},{10,1... | collective-permute-start | bytes 98312 | tf_op jit(solution)/shard_map/ppermute | solution.py:39
  35.4 5.3 %collective-permute-start.1 = (f32[8,4,256]{2,0,1:T(8,128)S(1)}, f32[8,4,256]{2,0,1:T(8,128)S(1)}, u32[]{:S(2)}, u32[]{:S(2)}) collective-permute-start(f32[8,4,256]{2,0,1:T(8,128)S(1)} %get-tuple-element.23), channel_id=1, source_target_pairs={{1,0},{2,1},{3,2},{4,3},{5,4},{6,5},{7,6},{0,7},{9,8},{10,9},{11,1... | collective-permute-start | bytes 98312 | tf_op jit(solution)/shard_map/ppermute | solution.py:41
  49.5 19.7 %all-to-all-start.1 = ((f32[4,64,1,256]{3,0,2,1:T(4,128)}), f32[4,64,1,256]{3,0,2,1:T(4,128)S(1)}, u32[]{:S(2)}, u32[]{:S(2)}) async-start(f32[4,64,1,256]{3,0,2,1:T(4,128)} %fusion.80), calls=%async_computation.1 | async-start | bytes 524288 | tf_op jit(solution)/shard_map/all_to_all | solution.py:138
  55.1 0.7 copy-start.2
  73.5 0.7 copy-start.3
where the time goes:
time: 106 us; the launch traced here: 105 us
  local copies, waits for them, and re-layouts  32.4 us (31%)
  starting transfers between devices  30.7 us (29%)
  waiting for transfers between devices  26.3 us (25%)
  matrix products  8.19 us (8%)
  other arithmetic  6.57 us (6%)
    all_to_all x1, starting transfers between devices, sent_to_all(): lax.all_to_all(jnp.broadcast_to(shard[None], (peers, *shard.shape)), axis...  17.7 us
    all_to_all x1, waiting for transfers between devices, on_device(): lax.all_to_all(shaped, 'wide', split_axis=1, concat_axis=0, tiled=True)  13.3 us
    gather x6, local copies, waits for them, and re-layouts, react_cells(): jnp.take(cell_block, first_ids, axis=0)  12.9 us
    gather x6, local copies, waits for them, and re-layouts, react_cells(): jnp.take(cell_block, second_ids, axis=0)  12.7 us
    all_to_all x1, waiting for transfers between devices, sent_to_all(): lax.all_to_all(jnp.broadcast_to(shard[None], (peers, *shard.shape)), axis...  12.5 us
    dot_general x6, matrix products, react_cells(): jnp.dot(net_matrix, rate_values, precision=lax.Precision.HIGHEST)  8.19 us
    all_to_all x1, starting transfers between devices, on_device(): lax.all_to_all(shaped, 'wide', split_axis=1, concat_axis=0, tiled=True)  5.6 us
    ppermute x1, starting transfers between devices, padded(): lax.ppermute(head, axis, [((i + 1) % count, i) for i in range(count)])  4.27 us
  transfers between devices with their start and end apart: 4, of which 3 were waited for; matrix products, arithmetic and copies ran while one was open for 1% of the time, Pallas kernels for 0%

commit v1 on v0

v1 whole, which is shorter than its diff:
```python
import jax
import jax.numpy as jnp
from jax import lax
from jax.experimental import pallas as pl
from jax.experimental.pallas import tpu as pltpu
from jax.sharding import PartitionSpec as P

S = 256
SUB = 2
SECTIONS = 6
DIFFUSION = 0.1
CHEM_STEP = 0.02
RIM = 4
SENT = jnp.float16


def minmod(first_jump, second_jump):
    return jnp.maximum(0.0, jnp.minimum(first_jump, second_jump)) + jnp.minimum(
        0.0, jnp.maximum(first_jump, second_jump)
    )


def face_flux(here, there, slope_here, slope_there, jump, speed):
    forward = speed >= 0.0
    value = jnp.where(forward, here, there)
    slope = jnp.where(forward, slope_here, slope_there)
    reach = jnp.where(forward, 0.5 - 0.5 * speed, -0.5 - 0.5 * speed)
    return speed * (value + reach * slope) - DIFFUSION * jump


def sweep_rows(rows, winds):
    count = len(rows)
    jumps = [rows[i + 1] - rows[i] for i in range(count - 1)]
    slopes = [None] + [minmod(jumps[i - 1], jumps[i]) for i in range(1, count - 1)]
    fluxes = [None] + [
        face_flux(
            rows[i], rows[i + 1], slopes[i], slopes[i + 1], jumps[i], 0.5 * (winds[i] + winds[i + 1])
        )
        for i in range(1, count - 2)
    ]
    return [rows[i] - (fluxes[i] - fluxes[i - 1]) for i in range(2, count - 2)]


def sweep_lanes(row, wind, last):
    lanes = row.shape[-1]
    axis = row.ndim - 1

    def ahead(x):
        return pltpu.roll(x, lanes - 1, axis)

    def behind(x):
        return pltpu.roll(x, 1, axis)

    there = ahead(row)
    jump = jnp.where(last, 0.0, there - row)
    slope = minmod(behind(jump), jump)
    speed = jnp.where(last, 0.0, 0.5 * (wind + ahead(wind)))
    flux = face_flux(row, there, slope, ahead(slope), jump, speed)
    return row - (flux - behind(flux))


def transport_kernel(own_ref, above_ref, below_ref, winds_ref, out_ref, ext_ref, speed_ref):
    rows, groups, lanes = own_ref.shape
    half = rows // 2
    count = half + 2 * RIM
    ext_ref[0:RIM, 0:groups] = above_ref[...]
    ext_ref[RIM:count, 0:groups] = own_ref[0 : half + RIM]
    ext_ref[0 : count - RIM, groups:] = own_ref[half - RIM : rows]
    ext_ref[count - RIM : count, groups:] = below_ref[...]
    upper = lax.broadcasted_iota(jnp.int32, (2 * groups, lanes), 0) < groups
    last = lax.broadcasted_iota(jnp.int32, (2 * groups, lanes), 1) == lanes - 1
    speed_ref[...] = winds_ref[...].astype(jnp.float32)

    def wind_row(plane, at):
        if at < RIM:
            row, place = rows - RIM + at, SUB * 2 + plane
        elif at < RIM + rows:
            row, place = at - RIM, plane
        else:
            row, place = at - RIM - rows, SUB * 2 + plane
        return jnp.broadcast_to(speed_ref[row, place : place + 1], (2 * groups, lanes))

    def wind(plane, at):
        return jnp.where(upper, wind_row(plane, at), wind_row(plane, at + half))

    field = [ext_ref[i] for i in range(count)]
    first = 0
    for substep in range(SUB):
        winds = [wind(2 * substep, first + i) for i in range(len(field))]
        field = sweep_rows(field, winds)
        first += 2
        field = [
            sweep_lanes(row, wind(2 * substep + 1, first + i), last) for i, row in enumerate(field)
        ]
    for i, row in enumerate(field):
        out_ref[i] = row[0:groups].astype(out_ref.dtype)
        out_ref[half + i] = row[groups:].astype(out_ref.dtype)


def transport(own, above, below, winds):
    rows, groups, lanes = own.shape
    return pl.pallas_call(
        transport_kernel,
        out_shape=jax.ShapeDtypeStruct(own.shape, jnp.float32),
        in_specs=[pl.BlockSpec(memory_space=pltpu.VMEM)] * 4,
        out_specs=pl.BlockSpec(memory_space=pltpu.VMEM),
        scratch_shapes=[
            pltpu.VMEM((rows // 2 + 2 * RIM, 2 * groups, lanes), jnp.float32),
            pltpu.VMEM(winds.shape, jnp.float32),
        ],
        cost_estimate=pl.CostEstimate(flops=4_000_000_000, bytes_accessed=600_000, transcendentals=0),
        name="transport",
    )(own, above, below, winds)


def tables_kernel(rates_ref, reactants_ref, products_ref, pick_ref, net_ref, rate_ref):
    count = rates_ref.shape[-1]
    ids = lax.broadcasted_iota(jnp.int32, (S, count), 0)

    def one_hot(ref, place):
        return jnp.where(ids == ref[place : place + 1, :], 1.0, 0.0)

    first, second = one_hot(reactants_ref, 0), one_hot(reactants_ref, 1)
    pick_ref[0:count] = first.T.astype(jnp.bfloat16)
    pick_ref[count:] = second.T.astype(jnp.bfloat16)
    net = one_hot(products_ref, 0) + one_hot(products_ref, 1) - first - second
    net_ref[...] = net.astype(jnp.bfloat16)
    rate_ref[...] = jnp.broadcast_to(rates_ref[...], (128, count)).T


def tables(rate_constants, reactants, products):
    count = rate_constants.shape[0]
    return pl.pallas_call(
        tables_kernel,
        out_shape=(
            jax.ShapeDtypeStruct((2 * count, S), jnp.bfloat16),
            jax.ShapeDtypeStruct((S, count), jnp.bfloat16),
            jax.ShapeDtypeStruct((count, 128), jnp.float32),
        ),
        in_specs=[pl.BlockSpec(memory_space=pltpu.VMEM)] * 3,
        out_specs=(pl.BlockSpec(memory_space=pltpu.VMEM),) * 3,
        cost_estimate=pl.CostEstimate(flops=4_000_000_000, bytes_accessed=2_000_000, transcendentals=0),
        name="tables",
    )(rate_constants.reshape(1, count), reactants.T, products.T)


def two_terms(x):
    high = x.astype(jnp.bfloat16)
    return high, (x - high.astype(jnp.float32)).astype(jnp.bfloat16)


def chemistry_kernel(cells_ref, pick_ref, net_ref, rate_ref, out_ref):
    count = net_ref.shape[1]
    chunk = 256
    cells = cells_ref[...].reshape(S, cells_ref.shape[-1]).astype(jnp.float32)

    def dot(a, b):
        return jnp.dot(a, b, preferred_element_type=jnp.float32)

    def section(_, cells):
        high, low = two_terms(cells)
        change = jnp.zeros_like(cells)
        for at in range(0, count, chunk):
            here, there = slice(at, at + chunk), slice(count + at, count + at + chunk)
            first = dot(pick_ref[here], high) + dot(pick_ref[here], low)
            second = dot(pick_ref[there], high) + dot(pick_ref[there], low)
            constant = rate_ref[here]
            rate = jnp.concatenate([constant, constant], 1) * first * second
            rate_high, rate_low = two_terms(rate)
            change = change + dot(net_ref[:, here], rate_high) + dot(net_ref[:, here], rate_low)
        return cells + CHEM_STEP * change

    cells = lax.fori_loop(0, SECTIONS, section, cells)
    out_ref[...] = cells.reshape(out_ref.shape)


def chemistry(cells, pick, net, rate):
    columns = cells.shape[-1]
    return pl.pallas_call(
        chemistry_kernel,
        out_shape=jax.ShapeDtypeStruct((S, 1, columns), jnp.float32),
        in_specs=[pl.BlockSpec(memory_space=pltpu.VMEM)] * 4,
        out_specs=pl.BlockSpec(memory_space=pltpu.VMEM),
        cost_estimate=pl.CostEstimate(flops=4_000_000_000, bytes_accessed=2_000_000, transcendentals=0),
        name="chemistry",
    )(cells, pick, net, rate)


def on_device(concentrations, wind_speeds, rate_constants, reactants, products):
    groups, _, columns = concentrations.shape
    wide, narrow = lax.axis_size("wide"), lax.axis_size("narrow")
    at_wide, at_narrow = lax.axis_index("wide"), lax.axis_index("narrow")
    above, below = (at_narrow - 1) % narrow, (at_narrow + 1) % narrow
    planes = wind_speeds.reshape(SUB * 2, columns)
    own = concentrations.swapaxes(0, 1)
    wind_row = planes.astype(jnp.float32)[None]
    down = jnp.concatenate([own[-RIM:], wind_row], 0)
    up = jnp.concatenate([own[:RIM], wind_row], 0)
    peers = lax.broadcasted_iota(jnp.int32, (narrow, 1, 1, 1), 0)
    rims = lax.all_to_all(jnp.where(peers == below, down[None], up[None]), "narrow", 0, 0, tiled=True)
    from_above = lax.dynamic_index_in_dim(rims, above, 0, False)
    from_below = lax.dynamic_index_in_dim(rims, below, 0, False)
    rim_row = jnp.where(at_wide < wide // 2, from_below[RIM], from_above[RIM]).astype(planes.dtype)
    sent = jnp.concatenate([planes, rim_row], 0)
    winds = lax.all_to_all(
        jnp.broadcast_to(sent[None], (wide, *sent.shape)), "wide", 0, 0, tiled=True
    )
    pick, net, rate = tables(rate_constants, reactants, products)
    moved = transport(own, from_above[:RIM], from_below[:RIM], winds)
    cells = lax.all_to_all(moved.astype(SENT), "wide", 0, 0, tiled=True)
    return chemistry(cells.astype(jnp.float32), pick, net, rate)


def solution(mesh):
    return jax.shard_map(
        on_device,
        mesh=mesh,
        in_specs=(
            P("wide", "narrow", None),
            P(None, None, ("narrow", "wide"), None),
            P(),
            P(),
            P(),
        ),
        out_specs=P(None, ("narrow", "wide"), None),
        check_vma=False,
    )
```

time: 106 us -> 87 us (0.82)
  local copies, waits for them, and re-layouts: 32.4 us -> 4.44 us
  Pallas kernels: 0 us -> 20 us
  matrix products: 8.19 us -> 0 us
  other arithmetic: 6.57 us -> 3.2 us
  waiting for transfers between devices: 26.3 us -> 28.8 us
    gather x12 -> x0, local copies, waits for them, and re-layouts: 25.5 us -> none  [the longest x6 12.9 us: react_cells(): jnp.take(cell_block, first_ids, axis=0)]
    pallas_call x0 -> x3, Pallas kernels: none -> 20 us  [the longest x1 9.44 us: chemistry(): pl.pallas_call(chemistry_kernel, out_shape=jax.ShapeDtypeStruct((S, 1, co...]
    dot_general x6 -> x0, matrix products: 8.19 us -> none  [react_cells(): jnp.dot(net_matrix, rate_values, precision=lax.Precision.HIGHEST)]
    ppermute x2 -> x0, starting transfers between devices: 7.39 us -> none  [the longest x1 4.27 us: padded(): lax.ppermute(head, axis, [((i + 1) % count, i) for i in range(count)])]
    all_to_all x2 -> x3, starting transfers between devices: 23.3 us -> 30 us  [the longest x1 17.5 us: on_device(): lax.all_to_all(jnp.broadcast_to(sent[None], (wide, *sent.shape)), 'wide',...]
    all_to_all x2 -> x3, waiting for transfers between devices: 25.8 us -> 28.8 us  [the longest x1 12.8 us: on_device(): lax.all_to_all(jnp.broadcast_to(sent[None], (wide, *sent.shape)), 'wide',...]
    convert_element_type x1 -> x3, other arithmetic: 0.04 us -> 2.41 us  [the longest x1 1.65 us: on_device(): cells = lax.all_to_all(moved.astype(SENT), 'wide', 0, 0, tiled=True)]
    sub x9 -> x0, other arithmetic: 1.6 us -> none  [the longest x4 0.64 us: sweep_axis(): take_range(extended, 1, length, along)]
  transfers between devices with their start and end apart: 4 -> 3, of which waited for: 3 -> 3; matrix products, arithmetic and copies ran while one was open for 1% -> 1% of each run, Pallas kernels for 0% -> 3%
where the time goes in v1:
time: 87 us; the launch traced here: 86.5 us
  starting transfers between devices  30 us (34%)
  waiting for transfers between devices  28.8 us (33%)
  Pallas kernels  20 us (23%)
  local copies, waits for them, and re-layouts  4.44 us (5%)
  other arithmetic  3.2 us (4%)
    all_to_all x1, starting transfers between devices, on_device(): lax.all_to_all(jnp.broadcast_to(sent[None], (wide, *sent.shape)), 'wide',...  17.5 us
    all_to_all x1, waiting for transfers between devices, on_device(): lax.all_to_all(jnp.broadcast_to(sent[None], (wide, *sent.shape)), 'wide',...  12.8 us
    all_to_all x1, waiting for transfers between devices, on_device(): cells = lax.all_to_all(moved.astype(SENT), 'wide', 0, 0, tiled=True)  10.4 us
    pallas_call x1, Pallas kernels, chemistry(): pl.pallas_call(chemistry_kernel, out_shape=jax.ShapeDtypeStruct((S, 1, co...  9.44 us
    pallas_call x1, Pallas kernels, transport(): pl.pallas_call(transport_kernel, out_shape=jax.ShapeDtypeStruct(own.shape...  8.26 us
    all_to_all x1, starting transfers between devices, on_device(): lax.all_to_all(jnp.where(peers == below, down[None], up[None]), 'narrow',...  6.65 us
    all_to_all x1, starting transfers between devices, on_device(): cells = lax.all_to_all(moved.astype(SENT), 'wide', 0, 0, tiled=True)  5.92 us
    all_to_all x1, waiting for transfers between devices, on_device(): lax.all_to_all(jnp.where(peers == below, down[None], up[None]), 'narrow',...  5.58 us
  transfers between devices with their start and end apart: 3, of which 3 were waited for; matrix products, arithmetic and copies ran while one was open for 1% of the time, Pallas kernels for 3%

profile of v1, /device:TPU:1, one launch (start us, length us, event | category | flops | bytes accessed | tf_op | source)
XLA Modules:
  0.0 86.5 jit_solution(6885761943430458759)
XLA Ops:
  0.0 0.0 copy-start.2
  0.0 0.7 copy-done.2
  0.7 1.1 %copy.8 = f32[4,64,256]{2,0,1:T(4,128)S(1)} copy(f32[4,64,256]{2,1,0:T(8,128)} %param.5) | data formatting | bytes 524288 | tf_op args[0]
  1.8 0.0 copy-start
  1.9 0.8 broadcast_select_fusion
  2.6 0.0 copy-done
  2.6 6.6 %all-to-all-start = ((f32[8,5,4,256]{3,2,1,0:T(4,128)}), f32[8,5,4,256]{3,2,1,0:T(4,128)S(1)}, u32[]{:S(2)}, u32[]{:S(2)}) async-start(f32[8,5,4,256]{3,2,1,0:T(4,128)} %broadcast_select_fusion), calls=%async_computation | async-start | bytes 327680 | tf_op jit(solution)/shard_map/all_to_all | solution.py:200
  9.3 5.6 %all-to-all-done = f32[8,5,4,256]{3,2,1,0:T(4,128)S(1)} async-done(((f32[8,5,4,256]{3,2,1,0:T(4,128)}), f32[8,5,4,256]{3,2,1,0:T(4,128)S(1)}, u32[]{:S(2)}, u32[]{:S(2)}) %all-to-all-start) | async-done | bytes 163872 | tf_op jit(solution)/shard_map/all_to_all | solution.py:200
  14.9 0.7 broadcast_in_dim.36
  15.6 0.0 copy-start.3
  15.6 17.5 %all-to-all-start.1 = ((bf16[64,8,256]{2,1,0:T(8,128)(2,1)}), bf16[64,8,256]{2,1,0:T(8,128)(2,1)S(1)}, u32[]{:S(2)}, u32[]{:S(2)}) async-start(bf16[64,8,256]{2,1,0:T(8,128)(2,1)} %broadcast_in_dim.36), calls=%async_computation.1 | async-start | bytes 524288 | tf_op jit(solution)/shard_map/all_to_all | solution.py:205
  33.1 0.0 copy-done.3
  33.1 0.6 reshape.36.rates_ref
  33.7 0.6 dynamic-slice_bitcast_fusion
  34.3 12.8 %all-to-all-done.1.winds_ref = bf16[64,8,256]{2,1,0:T(8,128)(2,1)S(1)} async-done(((bf16[64,8,256]{2,1,0:T(8,128)(2,1)}), bf16[64,8,256]{2,1,0:T(8,128)(2,1)S(1)}, u32[]{:S(2)}, u32[]{:S(2)}) %all-to-all-start.1) | async-done | bytes 262176 | tf_op jit(solution)/shard_map/all_to_all | solution.py:205
  47.1 0.0 copy-start.1
  47.1 0.7 copy-done.1
  47.8 8.3 %transport.1 = f32[64,4,256]{2,1,0:T(4,128)} custom-call(f32[64,4,256]{2,1,0:T(4,128)} %bitcast.16, f32[4,4,256]{2,1,0:T(4,128)} %get-tuple-element.14.above_ref, f32[4,4,256]{2,1,0:T(4,128)} %get-tuple-element.13.below_ref, bf16[64,8,256]{2,1,0:T(8,128)(2,1)} %copy-done.1), custom_call_target="tpu_custom_call" | custom-call | flops 4000000000 | bytes 600000 | tf_op jit(solution)/shard_map/transport/pallas_call | solution.py:102
  56.0 1.6 %convert_element_type.29 = f16[64,4,256]{2,1,0:T(4,128)(2,1)} convert(f32[64,4,256]{2,1,0:T(4,128)} %transport.1) | non-fusion elementwise | flops 65536 | bytes 393216 | tf_op jit(solution)/shard_map/convert_element_type | solution.py:210
  57.7 5.9 %all-to-all-start.2 = ((f16[64,4,256]{2,1,0:T(4,128)(2,1)}), f16[64,4,256]{2,1,0:T(4,128)(2,1)S(1)}, u32[]{:S(2)}, u32[]{:S(2)}) async-start(f16[64,4,256]{2,1,0:T(4,128)(2,1)} %convert_element_type.29), calls=%async_computation.2 | async-start | bytes 262144 | tf_op jit(solution)/shard_map/all_to_all | solution.py:210
  63.6 2.3 %tables.1 = (bf16[1536,256]{1,0:T(8,128)(2,1)}, bf16[256,768]{1,0:T(8,128)(2,1)}, f32[768,128]{1,0:T(8,128)}) custom-call(f32[1,768]{1,0:T(1,128)} %reshape.36.rates_ref, s32[2,768]{1,0:T(2,128)} %bitcast.17, s32[2,768]{1,0:T(2,128)} %bitcast.18), custom_call_target="tpu_custom_call" | custom-call | flops 4000000000 | bytes 2000000 | tf_op jit(solution)/shard_map/tables/pallas_call | solution.py:133
  65.9 10.4 %all-to-all-done.2 = f16[64,4,256]{2,1,0:T(4,128)(2,1)S(1)} async-done(((f16[64,4,256]{2,1,0:T(4,128)(2,1)}), f16[64,4,256]{2,1,0:T(4,128)(2,1)S(1)}, u32[]{:S(2)}, u32[]{:S(2)}) %all-to-all-start.2) | async-done | bytes 131104 | tf_op jit(solution)/shard_map/all_to_all | solution.py:210
  76.3 0.7 convert_element_type.30.cells_ref
  77.1 9.4 %chemistry.1 = f32[256,1,256]{2,1,0:T(1,128)} custom-call(f32[64,4,256]{2,1,0:T(4,128)} %convert_element_type.30.cells_ref, bf16[1536,256]{1,0:T(8,128)(2,1)} %get-tuple-element.8.pick_ref, bf16[256,768]{1,0:T(8,128)(2,1)} %get-tuple-element.9.net_ref, f32[768,128]{1,0:T(8,128)} %get-tuple-element.10.rate_ref), custom_call_target="tpu_custom_call" | custom-call | flops 4000000000 | bytes 2000000 | tf_op jit(solution)/shard_map/chemistry/pallas_call | solution.py:179
  (7 shorter events, 0.1 us)
Async XLA Ops:
  0.0 0.7 copy-start.2
  1.8 0.8 copy-start
  2.6 12.3 %all-to-all-start = ((f32[8,5,4,256]{3,2,1,0:T(4,128)}), f32[8,5,4,256]{3,2,1,0:T(4,128)S(1)}, u32[]{:S(2)}, u32[]{:S(2)}) async-start(f32[8,5,4,256]{3,2,1,0:T(4,128)} %broadcast_select_fusion), calls=%async_computation | async-start | bytes 327680 | tf_op jit(solution)/shard_map/all_to_all | solution.py:200
  15.6 17.5 %copy-start.3 = (f32[768]{0:T(1024)S(1)}, f32[768]{0:T(1024)}, u32[]{:S(2)}) copy-start(f32[768]{0:T(1024)} %param.7) | copy-start | bytes 9220
  15.6 31.4 %all-to-all-start.1 = ((bf16[64,8,256]{2,1,0:T(8,128)(2,1)}), bf16[64,8,256]{2,1,0:T(8,128)(2,1)S(1)}, u32[]{:S(2)}, u32[]{:S(2)}) async-start(bf16[64,8,256]{2,1,0:T(8,128)(2,1)} %broadcast_in_dim.36), calls=%async_computation.1 | async-start | bytes 524288 | tf_op jit(solution)/shard_map/all_to_all | solution.py:205
  47.1 0.7 copy-start.1
  57.7 18.7 %all-to-all-start.2 = ((f16[64,4,256]{2,1,0:T(4,128)(2,1)}), f16[64,4,256]{2,1,0:T(4,128)(2,1)S(1)}, u32[]{:S(2)}, u32[]{:S(2)}) async-start(f16[64,4,256]{2,1,0:T(4,128)(2,1)} %convert_element_type.29), calls=%async_computation.2 | async-start | bytes 262144 | tf_op jit(solution)/shard_map/all_to_all | solution.py:210

commit v2 on v1

--- a/solution.py
+++ b/solution.py
@@ -1,3 +1,5 @@
+import functools
+
 import jax
 import jax.numpy as jnp
 from jax import lax
@@ -28,70 +30,113 @@
     return speed * (value + reach * slope) - DIFFUSION * jump
 
 
-def sweep_rows(rows, winds):
+def sweep_rows(rows, speeds):
     count = len(rows)
     jumps = [rows[i + 1] - rows[i] for i in range(count - 1)]
     slopes = [None] + [minmod(jumps[i - 1], jumps[i]) for i in range(1, count - 1)]
     fluxes = [None] + [
-        face_flux(
-            rows[i], rows[i + 1], slopes[i], slopes[i + 1], jumps[i], 0.5 * (winds[i] + winds[i + 1])
-        )
+        face_flux(rows[i], rows[i + 1], slopes[i], slopes[i + 1], jumps[i], speeds[i])
         for i in range(1, count - 2)
     ]
     return [rows[i] - (fluxes[i] - fluxes[i - 1]) for i in range(2, count - 2)]
 
 
-def sweep_lanes(row, wind, last):
-    lanes = row.shape[-1]
-    axis = row.ndim - 1
-
-    def ahead(x):
-        return pltpu.roll(x, lanes - 1, axis)
-
-    def behind(x):
-        return pltpu.roll(x, 1, axis)
-
-    there = ahead(row)
-    jump = jnp.where(last, 0.0, there - row)
-    slope = minmod(behind(jump), jump)
-    speed = jnp.where(last, 0.0, 0.5 * (wind + ahead(wind)))
-    flux = face_flux(row, there, slope, ahead(slope), jump, speed)
-    return row - (flux - behind(flux))
-
-
-def transport_kernel(own_ref, above_ref, below_ref, winds_ref, out_ref, ext_ref, speed_ref):
+def maps_kernel(pick_ref, shift_ref, face_ref, *, rows, groups, planes):
+    half = rows // 2
+    count = pick_ref.shape[1]
+    sources = pick_ref.shape[2]
+    lanes = shift_ref.shape[0]
+    at = lax.broadcasted_iota(jnp.int32, (count, sources), 0)
+    source = lax.broadcasted_iota(jnp.int32, (count, sources), 1)
+    row = at // (2 * groups) + jnp.where(at % (2 * groups) < groups, 0, half)
+    before, after = row < RIM, row >= RIM + rows
+    place = row - RIM + jnp.where(before, rows, 0) - jnp.where(after, rows, 0)
+    start = place * (2 * planes) + jnp.where(before | after, planes, 0)
+    for plane in range(planes):
+        weight = 1.0 if plane % 2 else 0.5
+        pick_ref[plane] = jnp.where(source == start + plane, weight, 0.0).astype(jnp.bfloat16)
+    here = lax.broadcasted_iota(jnp.int32, (lanes, lanes), 0)
+    there = lax.broadcasted_iota(jnp.int32, (lanes, lanes), 1)
+    for i, step in enumerate((-2, -1, 1, 2)):
+        moved = jnp.clip(there + step, 0, lanes - 1)
+        shift_ref[:, i * lanes : (i + 1) * lanes] = jnp.where(here == moved, 1.0, 0.0).astype(
+            jnp.bfloat16
+        )
+    below = ((here == there) | (here == there - 1)) & (there > 0)
+    above = ((here == there) | (here == there + 1)) & (there < lanes - 1)
+    face_ref[:, :lanes] = jnp.where(below, 0.5, 0.0).astype(jnp.bfloat16)
+    face_ref[:, lanes:] = jnp.where(above, 0.5, 0.0).astype(jnp.bfloat16)
+
+
+def maps(rows, groups, lanes):
+    planes = SUB * 2
+    count = (rows // 2 + 2 * RIM) * 2 * groups
+    return pl.pallas_call(
+        functools.partial(maps_kernel, rows=rows, groups=groups, planes=planes),
+        out_shape=(
+            jax.ShapeDtypeStruct((planes, count, rows * planes * 2), jnp.bfloat16),
+            jax.ShapeDtypeStruct((lanes, 4 * lanes), jnp.bfloat16),
+            jax.ShapeDtypeStruct((lanes, 2 * lanes), jnp.bfloat16),
+        ),
+        out_specs=(pl.BlockSpec(memory_space=pltpu.VMEM),) * 3,
+        cost_estimate=pl.CostEstimate(flops=2_000_000_000, bytes_accessed=2_000_000, transcendentals=0),
+        compiler_params=pltpu.CompilerParams(vmem_limit_bytes=8 << 20),
+        name="maps",
+    )()
+
+
+def matmul(a, b):
+    return jnp.dot(a, b, preferred_element_type=jnp.float32)
+
+
+def two_terms(x):
+    high = x.astype(jnp.bfloat16)
+    return high, (x - high.astype(jnp.float32)).astype(jnp.bfloat16)
+
+
+def transport_kernel(
+    own_ref, above_ref, below_ref, winds_ref, pick_ref, shift_ref, face_ref, out_ref,
+    ext_ref, moved_ref, speed_ref,
+):
     rows, groups, lanes = own_ref.shape
+    tall = 2 * groups
     half = rows // 2
     count = half + 2 * RIM
     ext_ref[0:RIM, 0:groups] = above_ref[...]
     ext_ref[RIM:count, 0:groups] = own_ref[0 : half + RIM]
     ext_ref[0 : count - RIM, groups:] = own_ref[half - RIM : rows]
     ext_ref[count - RIM : count, groups:] = below_ref[...]
-    upper = lax.broadcasted_iota(jnp.int32, (2 * groups, lanes), 0) < groups
-    last = lax.broadcasted_iota(jnp.int32, (2 * groups, lanes), 1) == lanes - 1
-    speed_ref[...] = winds_ref[...].astype(jnp.float32)
-
-    def wind_row(plane, at):
-        if at < RIM:
-            row, place = rows - RIM + at, SUB * 2 + plane
-        elif at < RIM + rows:
-            row, place = at - RIM, plane
-        else:
-            row, place = at - RIM - rows, SUB * 2 + plane
-        return jnp.broadcast_to(speed_ref[row, place : place + 1], (2 * groups, lanes))
-
-    def wind(plane, at):
-        return jnp.where(upper, wind_row(plane, at), wind_row(plane, at + half))
+    winds = winds_ref[...].reshape(rows * tall, lanes)
 
     field = [ext_ref[i] for i in range(count)]
     first = 0
     for substep in range(SUB):
-        winds = [wind(2 * substep, first + i) for i in range(len(field))]
-        field = sweep_rows(field, winds)
+        low, high = first * tall, (first + len(field)) * tall
+        halves = matmul(pick_ref[2 * substep, low:high], winds)
+        speeds = [
+            halves[i * tall : (i + 1) * tall] + halves[(i + 1) * tall : (i + 2) * tall]
+            for i in range(len(field) - 1)
+        ]
+        field = sweep_rows(field, speeds)
         first += 2
-        field = [
-            sweep_lanes(row, wind(2 * substep + 1, first + i), last) for i, row in enumerate(field)
-        ]
+        size = len(field) * tall
+        low = first * tall
+        across = matmul(pick_ref[2 * substep + 1, low : low + size], winds).astype(jnp.bfloat16)
+        speed_ref[0:size] = matmul(across, face_ref[...])
+        upper, lower = two_terms(jnp.concatenate(field, 0))
+        moved_ref[0:size] = matmul(upper, shift_ref[...]) + matmul(lower, shift_ref[...])
+        swept = []
+        for i, row in enumerate(field):
+            part = slice(i * tall, (i + 1) * tall)
+            back2, back1, next1, next2 = (
+                moved_ref[part, k * lanes : (k + 1) * lanes] for k in range(4)
+            )
+            jumps = [back1 - back2, row - back1, next1 - row, next2 - next1]
+            slopes = [minmod(jumps[k], jumps[k + 1]) for k in range(3)]
+            low_flux = face_flux(back1, row, slopes[0], slopes[1], jumps[1], speed_ref[part, :lanes])
+            high_flux = face_flux(row, next1, slopes[1], slopes[2], jumps[2], speed_ref[part, lanes:])
+            swept.append(row - (high_flux - low_flux))
+        field = swept
     for i, row in enumerate(field):
         out_ref[i] = row[0:groups].astype(out_ref.dtype)
         out_ref[half + i] = row[groups:].astype(out_ref.dtype)
@@ -99,18 +144,23 @@
 
 def transport(own, above, below, winds):
     rows, groups, lanes = own.shape
+    tall = 2 * groups
+    size = (rows // 2 + 2 * RIM) * tall
+    constants = maps(rows, groups, lanes)
     return pl.pallas_call(
         transport_kernel,
         out_shape=jax.ShapeDtypeStruct(own.shape, jnp.float32),
-        in_specs=[pl.BlockSpec(memory_space=pltpu.VMEM)] * 4,
+        in_specs=[pl.BlockSpec(memory_space=pltpu.VMEM)] * 7,
         out_specs=pl.BlockSpec(memory_space=pltpu.VMEM),
         scratch_shapes=[
-            pltpu.VMEM((rows // 2 + 2 * RIM, 2 * groups, lanes), jnp.float32),
-            pltpu.VMEM(winds.shape, jnp.float32),
+            pltpu.VMEM((rows // 2 + 2 * RIM, tall, lanes), jnp.float32),
+            pltpu.VMEM((size, 4 * lanes), jnp.float32),
+            pltpu.VMEM((size, 2 * lanes), jnp.float32),
         ],
         cost_estimate=pl.CostEstimate(flops=4_000_000_000, bytes_accessed=600_000, transcendentals=0),
+        compiler_params=pltpu.CompilerParams(vmem_limit_bytes=16 << 20),
         name="transport",
-    )(own, above, below, winds)
+    )(own, above, below, winds, *constants)
 
 
 def tables_kernel(rates_ref, reactants_ref, products_ref, pick_ref, net_ref, rate_ref):
@@ -140,34 +190,27 @@
         in_specs=[pl.BlockSpec(memory_space=pltpu.VMEM)] * 3,
         out_specs=(pl.BlockSpec(memory_space=pltpu.VMEM),) * 3,
         cost_estimate=pl.CostEstimate(flops=4_000_000_000, bytes_accessed=2_000_000, transcendentals=0),
+        compiler_params=pltpu.CompilerParams(vmem_limit_bytes=16 << 20),
         name="tables",
     )(rate_constants.reshape(1, count), reactants.T, products.T)
-
-
-def two_terms(x):
-    high = x.astype(jnp.bfloat16)
-    return high, (x - high.astype(jnp.float32)).astype(jnp.bfloat16)
 
 
 def chemistry_kernel(cells_ref, pick_ref, net_ref, rate_ref, out_ref):
     count = net_ref.shape[1]
     chunk = 256
     cells = cells_ref[...].reshape(S, cells_ref.shape[-1]).astype(jnp.float32)
-
-    def dot(a, b):
-        return jnp.dot(a, b, preferred_element_type=jnp.float32)
 
     def section(_, cells):
         high, low = two_terms(cells)
         change = jnp.zeros_like(cells)
         for at in range(0, count, chunk):
             here, there = slice(at, at + chunk), slice(count + at, count + at + chunk)
-            first = dot(pick_ref[here], high) + dot(pick_ref[here], low)
-            second = dot(pick_ref[there], high) + dot(pick_ref[there], low)
+            first = matmul(pick_ref[here], high) + matmul(pick_ref[here], low)
+            second = matmul(pick_ref[there], high) + matmul(pick_ref[there], low)
             constant = rate_ref[here]
             rate = jnp.concatenate([constant, constant], 1) * first * second
             rate_high, rate_low = two_terms(rate)
-            change = change + dot(net_ref[:, here], rate_high) + dot(net_ref[:, here], rate_low)
+            change = change + matmul(net_ref[:, here], rate_high) + matmul(net_ref[:, here], rate_low)
         return cells + CHEM_STEP * change
 
     cells = lax.fori_loop(0, SECTIONS, section, cells)
@@ -182,6 +225,7 @@
         in_specs=[pl.BlockSpec(memory_space=pltpu.VMEM)] * 4,
         out_specs=pl.BlockSpec(memory_space=pltpu.VMEM),
         cost_estimate=pl.CostEstimate(flops=4_000_000_000, bytes_accessed=2_000_000, transcendentals=0),
+        compiler_params=pltpu.CompilerParams(vmem_limit_bytes=16 << 20),
         name="chemistry",
     )(cells, pick, net, rate)
 

time: 87 us -> 76.8 us (0.88)
  Pallas kernels: 20 us -> 11.2 us
  other arithmetic: 3.2 us -> 1.55 us
  waiting for transfers between devices: 28.8 us -> 30.4 us
  local copies, waits for them, and re-layouts: 4.44 us -> 3.26 us
    pallas_call x1, Pallas kernels: 8.26 us -> 2.03 us  [transport(): pl.pallas_call(transport_kernel, out_shape=jax.ShapeDtypeStruct(own.shape...]
    pallas_call x1, Pallas kernels: 2.33 us -> 0.63 us  [tables(): pl.pallas_call(tables_kernel, out_shape=(jax.ShapeDtypeStruct((2 * count,...]
    all_to_all x1, waiting for transfers between devices: 10.4 us -> 12.1 us  [on_device(): cells = lax.all_to_all(moved.astype(SENT), 'wide', 0, 0, tiled=True)]
    unnamed x9 -> x7, local copies, waits for them, and re-layouts: 2.5 us -> 1.14 us
    pallas_call x1, Pallas kernels: 9.44 us -> 8.09 us  [chemistry(): pl.pallas_call(chemistry_kernel, out_shape=jax.ShapeDtypeStruct((S, 1, co...]
    convert_element_type x1, other arithmetic: 1.65 us -> 0.7 us  [on_device(): cells = lax.all_to_all(moved.astype(SENT), 'wide', 0, 0, tiled=True)]
  transfers between devices with their start and end apart: 3 -> 3, of which waited for: 3 -> 3; matrix products, arithmetic and copies ran while one was open for 1% -> 1% of each run, Pallas kernels for 3% -> 1%
where the time goes in v2:
time: 76.8 us; the launch traced here: 76.5 us
  waiting for transfers between devices  30.4 us (40%)
  starting transfers between devices  29.9 us (39%)
  Pallas kernels  11.2 us (15%)
  local copies, waits for them, and re-layouts  3.26 us (4%)
  other arithmetic  1.55 us (2%)
    all_to_all x1, starting transfers between devices, on_device(): lax.all_to_all(jnp.broadcast_to(sent[None], (wide, *sent.shape)), 'wide',...  17.3 us
    all_to_all x1, waiting for transfers between devices, on_device(): lax.all_to_all(jnp.broadcast_to(sent[None], (wide, *sent.shape)), 'wide',...  13.4 us
    all_to_all x1, waiting for transfers between devices, on_device(): cells = lax.all_to_all(moved.astype(SENT), 'wide', 0, 0, tiled=True)  12.1 us
    pallas_call x1, Pallas kernels, chemistry(): pl.pallas_call(chemistry_kernel, out_shape=jax.ShapeDtypeStruct((S, 1, co...  8.09 us
    all_to_all x1, starting transfers between devices, on_device(): lax.all_to_all(jnp.where(peers == below, down[None], up[None]), 'narrow',...  6.65 us
    all_to_all x1, starting transfers between devices, on_device(): cells = lax.all_to_all(moved.astype(SENT), 'wide', 0, 0, tiled=True)  5.92 us
    all_to_all x1, waiting for transfers between devices, on_device(): lax.all_to_all(jnp.where(peers == below, down[None], up[None]), 'narrow',...  4.92 us
    pallas_call x1, Pallas kernels, transport(): pl.pallas_call(transport_kernel, out_shape=jax.ShapeDtypeStruct(own.shape...  2.03 us
  transfers between devices with their start and end apart: 3, of which 3 were waited for; matrix products, arithmetic and copies ran while one was open for 1% of the time, Pallas kernels for 1%

profile of v2, /device:TPU:1, one launch (start us, length us, event | category | flops | bytes accessed | tf_op | source)
XLA Modules:
  0.0 76.5 jit_solution(16270137225711026168)
XLA Ops:
  0.0 0.0 copy-start.2
  0.0 1.1 %copy.8 = f32[4,64,256]{2,0,1:T(4,128)S(1)} copy(f32[4,64,256]{2,1,0:T(8,128)} %param.5) | data formatting | bytes 524288 | tf_op args[0]
  1.2 0.7 reshape.37
  1.9 0.8 broadcast_select_fusion
  2.6 6.6 %all-to-all-start = ((f32[8,5,4,256]{3,2,1,0:T(4,128)}), f32[8,5,4,256]{3,2,1,0:T(4,128)S(1)}, u32[]{:S(2)}, u32[]{:S(2)}) async-start(f32[8,5,4,256]{3,2,1,0:T(4,128)} %broadcast_select_fusion), calls=%async_computation | async-start | bytes 327680 | tf_op jit(solution)/shard_map/all_to_all | solution.py:244
  9.3 0.7 reshape.35
  10.0 4.9 %all-to-all-done = f32[8,5,4,256]{3,2,1,0:T(4,128)S(1)} async-done(((f32[8,5,4,256]{3,2,1,0:T(4,128)}), f32[8,5,4,256]{3,2,1,0:T(4,128)S(1)}, u32[]{:S(2)}, u32[]{:S(2)}) %all-to-all-start) | async-done | bytes 163872 | tf_op jit(solution)/shard_map/all_to_all | solution.py:244
  14.9 0.7 broadcast_in_dim.36
  15.6 17.3 %all-to-all-start.1 = ((bf16[64,8,256]{2,1,0:T(8,128)(2,1)}), bf16[64,8,256]{2,1,0:T(8,128)(2,1)S(1)}, u32[]{:S(2)}, u32[]{:S(2)}) async-start(bf16[64,8,256]{2,1,0:T(8,128)(2,1)} %broadcast_in_dim.36), calls=%async_computation.1 | async-start | bytes 524288 | tf_op jit(solution)/shard_map/all_to_all | solution.py:249
  33.0 0.0 copy-done.2
  33.0 0.5 maps.1
  33.5 13.4 %all-to-all-done.1.winds_ref = bf16[64,8,256]{2,1,0:T(8,128)(2,1)S(1)} async-done(((bf16[64,8,256]{2,1,0:T(8,128)(2,1)}), bf16[64,8,256]{2,1,0:T(8,128)(2,1)S(1)}, u32[]{:S(2)}, u32[]{:S(2)}) %all-to-all-start.1) | async-done | bytes 262176 | tf_op jit(solution)/shard_map/all_to_all | solution.py:249
  46.9 0.0 copy-start
  46.9 0.0 copy-start.1
  46.9 2.0 %transport.1 = f32[64,4,256]{2,1,0:T(4,128)S(1)} custom-call(f32[64,4,256]{2,1,0:T(4,128)S(1)} %bitcast.16, f32[4,4,256]{2,1,0:T(4,128)S(1)} %get-tuple-element.20.above_ref, f32[4,4,256]{2,1,0:T(4,128)S(1)} %get-tuple-element.19.below_ref, bf16[64,8,256]{2,1,0:T(8,128)(2,1)S(1)} %all-to-all-done.1.winds_ref, ...), custom_call_target="tpu_custom_call" | custom-call | flops 4000000000 | bytes 600000 | tf_op jit(solution)/shard_map/transport/pallas_call | solution.py:150
  49.0 0.7 convert_element_type.29
  49.7 5.9 %all-to-all-start.2 = ((f16[64,4,256]{2,1,0:T(4,128)(2,1)}), f16[64,4,256]{2,1,0:T(4,128)(2,1)S(1)}, u32[]{:S(2)}, u32[]{:S(2)}) async-start(f16[64,4,256]{2,1,0:T(4,128)(2,1)} %convert_element_type.29), calls=%async_computation.2 | async-start | bytes 262144 | tf_op jit(solution)/shard_map/all_to_all | solution.py:254
  55.6 0.0 copy-done
  55.6 0.0 copy-done.1
  55.6 0.6 tables.1
  56.2 12.1 %all-to-all-done.2 = f16[64,4,256]{2,1,0:T(4,128)(2,1)S(1)} async-done(((f16[64,4,256]{2,1,0:T(4,128)(2,1)}), f16[64,4,256]{2,1,0:T(4,128)(2,1)S(1)}, u32[]{:S(2)}, u32[]{:S(2)}) %all-to-all-start.2) | async-done | bytes 131104 | tf_op jit(solution)/shard_map/all_to_all | solution.py:254
  68.4 8.1 %chemistry.1 = f32[256,1,256]{2,1,0:T(1,128)} custom-call(f32[64,4,256]{2,1,0:T(4,128)S(1)} %convert_element_type.30.cells_ref, bf16[1536,256]{1,0:T(8,128)(2,1)S(1)} %get-tuple-element.14.pick_ref, bf16[256,768]{1,0:T(8,128)(2,1)S(1)} %get-tuple-element.15.net_ref, f32[768,128]{1,0:T(8,128)S(1)} %get-tuple-element.16.rate_ref), custom_call_target="tpu_custom_call" | custom-call | flops 4000000000 | bytes 2000000 | tf_op jit(solution)/shard_map/chemistry/pallas_call | solution.py:222
  (8 shorter events, 0.1 us)
Async XLA Ops:
  0.0 33.0 %copy-start.2 = (f32[768]{0:T(1024)S(1)}, f32[768]{0:T(1024)}, u32[]{:S(2)}) copy-start(f32[768]{0:T(1024)} %param.7) | copy-start | bytes 9220
  2.6 12.3 %all-to-all-start = ((f32[8,5,4,256]{3,2,1,0:T(4,128)}), f32[8,5,4,256]{3,2,1,0:T(4,128)S(1)}, u32[]{:S(2)}, u32[]{:S(2)}) async-start(f32[8,5,4,256]{3,2,1,0:T(4,128)} %broadcast_select_fusion), calls=%async_computation | async-start | bytes 327680 | tf_op jit(solution)/shard_map/all_to_all | solution.py:244
  15.6 31.3 %all-to-all-start.1 = ((bf16[64,8,256]{2,1,0:T(8,128)(2,1)}), bf16[64,8,256]{2,1,0:T(8,128)(2,1)S(1)}, u32[]{:S(2)}, u32[]{:S(2)}) async-start(bf16[64,8,256]{2,1,0:T(8,128)(2,1)} %broadcast_in_dim.36), calls=%async_computation.1 | async-start | bytes 524288 | tf_op jit(solution)/shard_map/all_to_all | solution.py:249
  46.9 8.7 %copy-start = (s32[768,2]{0,1:T(2,128)S(1)}, s32[768,2]{0,1:T(2,128)}, u32[]{:S(2)}) copy-start(s32[768,2]{0,1:T(2,128)} %param.8) | copy-start | bytes 18436
  46.9 8.7 %copy-start.1 = (s32[768,2]{0,1:T(2,128)S(1)}, s32[768,2]{0,1:T(2,128)}, u32[]{:S(2)}) copy-start(s32[768,2]{0,1:T(2,128)} %param.9) | copy-start | bytes 18436
  49.7 18.7 %all-to-all-start.2 = ((f16[64,4,256]{2,1,0:T(4,128)(2,1)}), f16[64,4,256]{2,1,0:T(4,128)(2,1)S(1)}, u32[]{:S(2)}, u32[]{:S(2)}) async-start(f16[64,4,256]{2,1,0:T(4,128)(2,1)} %convert_element_type.29), calls=%async_computation.2 | async-start | bytes 262144 | tf_op jit(solution)/shard_map/all_to_all | solution.py:254

commit v3 on v2

--- a/solution.py
+++ b/solution.py
@@ -48,10 +48,7 @@
     lanes = shift_ref.shape[0]
     at = lax.broadcasted_iota(jnp.int32, (count, sources), 0)
     source = lax.broadcasted_iota(jnp.int32, (count, sources), 1)
-    row = at // (2 * groups) + jnp.where(at % (2 * groups) < groups, 0, half)
-    before, after = row < RIM, row >= RIM + rows
-    place = row - RIM + jnp.where(before, rows, 0) - jnp.where(after, rows, 0)
-    start = place * (2 * planes) + jnp.where(before | after, planes, 0)
+    start = (at // (2 * groups) + jnp.where(at % (2 * groups) < groups, 0, half)) * planes
     for plane in range(planes):
         weight = 1.0 if plane % 2 else 0.5
         pick_ref[plane] = jnp.where(source == start + plane, weight, 0.0).astype(jnp.bfloat16)
@@ -68,13 +65,17 @@
     face_ref[:, lanes:] = jnp.where(above, 0.5, 0.0).astype(jnp.bfloat16)
 
 
+def wind_depth(rows):
+    return pl.cdiv((rows + 2 * RIM) * SUB * 2, 128) * 128
+
+
 def maps(rows, groups, lanes):
     planes = SUB * 2
     count = (rows // 2 + 2 * RIM) * 2 * groups
     return pl.pallas_call(
         functools.partial(maps_kernel, rows=rows, groups=groups, planes=planes),
         out_shape=(
-            jax.ShapeDtypeStruct((planes, count, rows * planes * 2), jnp.bfloat16),
+            jax.ShapeDtypeStruct((planes, count, wind_depth(rows)), jnp.bfloat16),
             jax.ShapeDtypeStruct((lanes, 4 * lanes), jnp.bfloat16),
             jax.ShapeDtypeStruct((lanes, 2 * lanes), jnp.bfloat16),
         ),
@@ -96,17 +97,28 @@
 
 def transport_kernel(
     own_ref, above_ref, below_ref, winds_ref, pick_ref, shift_ref, face_ref, out_ref,
-    ext_ref, moved_ref, speed_ref,
+    ext_ref, wind_ref, moved_ref, speed_ref,
 ):
     rows, groups, lanes = own_ref.shape
+    planes = winds_ref.shape[1]
     tall = 2 * groups
     half = rows // 2
     count = half + 2 * RIM
-    ext_ref[0:RIM, 0:groups] = above_ref[...]
+    above, below = above_ref[...], below_ref[...]
+    ext_ref[0:RIM, 0:groups] = above[:, :groups]
     ext_ref[RIM:count, 0:groups] = own_ref[0 : half + RIM]
     ext_ref[0 : count - RIM, groups:] = own_ref[half - RIM : rows]
-    ext_ref[count - RIM : count, groups:] = below_ref[...]
-    winds = winds_ref[...].reshape(rows * tall, lanes)
+    ext_ref[count - RIM : count, groups:] = below[:, :groups]
+    rim, inner = RIM * planes, rows * planes
+
+    def wind_rows(cells):
+        return cells.astype(jnp.float32).reshape(-1, lanes).astype(jnp.bfloat16)
+
+    wind_ref[0:rim] = wind_rows(above[:, groups:])
+    wind_ref[rim : rim + inner] = wind_rows(winds_ref[...])
+    wind_ref[rim + inner : 2 * rim + inner] = wind_rows(below[:, groups:])
+    wind_ref[2 * rim + inner :] = jnp.zeros((wind_ref.shape[0] - 2 * rim - inner, lanes), jnp.bfloat16)
+    winds = wind_ref[...]
 
     field = [ext_ref[i] for i in range(count)]
     first = 0
@@ -154,6 +166,7 @@
         out_specs=pl.BlockSpec(memory_space=pltpu.VMEM),
         scratch_shapes=[
             pltpu.VMEM((rows // 2 + 2 * RIM, tall, lanes), jnp.float32),
+            pltpu.VMEM((wind_depth(rows), lanes), jnp.bfloat16),
             pltpu.VMEM((size, 4 * lanes), jnp.float32),
             pltpu.VMEM((size, 2 * lanes), jnp.float32),
         ],
@@ -233,24 +246,19 @@
 def on_device(concentrations, wind_speeds, rate_constants, reactants, products):
     groups, _, columns = concentrations.shape
     wide, narrow = lax.axis_size("wide"), lax.axis_size("narrow")
-    at_wide, at_narrow = lax.axis_index("wide"), lax.axis_index("narrow")
-    above, below = (at_narrow - 1) % narrow, (at_narrow + 1) % narrow
-    planes = wind_speeds.reshape(SUB * 2, columns)
+    winds = lax.all_to_all(
+        jnp.broadcast_to(wind_speeds[None], (wide, *wind_speeds.shape)), "wide", 0, 0, tiled=True
+    ).reshape(wide, SUB * 2, columns)
     own = concentrations.swapaxes(0, 1)
-    wind_row = planes.astype(jnp.float32)[None]
-    down = jnp.concatenate([own[-RIM:], wind_row], 0)
-    up = jnp.concatenate([own[:RIM], wind_row], 0)
-    peers = lax.broadcasted_iota(jnp.int32, (narrow, 1, 1, 1), 0)
-    rims = lax.all_to_all(jnp.where(peers == below, down[None], up[None]), "narrow", 0, 0, tiled=True)
-    from_above = lax.dynamic_index_in_dim(rims, above, 0, False)
-    from_below = lax.dynamic_index_in_dim(rims, below, 0, False)
-    rim_row = jnp.where(at_wide < wide // 2, from_below[RIM], from_above[RIM]).astype(planes.dtype)
-    sent = jnp.concatenate([planes, rim_row], 0)
-    winds = lax.all_to_all(
-        jnp.broadcast_to(sent[None], (wide, *sent.shape)), "wide", 0, 0, tiled=True
-    )
+
+    def rim(part):
+        return jnp.concatenate([own[part], winds[part].astype(jnp.float32)], 1)
+
+    down = [(i, (i + 1) % narrow) for i in range(narrow)]
+    from_above = lax.ppermute(rim(slice(-RIM, None)), "narrow", down)
+    from_below = lax.ppermute(rim(slice(RIM)), "narrow", [(j, i) for i, j in down])
     pick, net, rate = tables(rate_constants, reactants, products)
-    moved = transport(own, from_above[:RIM], from_below[:RIM], winds)
+    moved = transport(own, from_above, from_below, winds)
     cells = lax.all_to_all(moved.astype(SENT), "wide", 0, 0, tiled=True)
     return chemistry(cells.astype(jnp.float32), pick, net, rate)
 

time: 76.8 us -> 71 us (0.924); the launches traced: 76.5 us -> 69.8 us
  waiting for transfers between devices: 30.4 us -> 25.2 us
  local copies, waits for them, and re-layouts: 3.26 us -> 1.77 us
  starting transfers between devices: 29.9 us -> 30.7 us
  other arithmetic: 1.55 us -> 0.78 us
    ppermute x0 -> x2, starting transfers between devices: none -> 7.39 us  [the longest x1 4.27 us: on_device(): lax.ppermute(rim(slice(RIM)), 'narrow', [(j, i) for i, j in down])]
    all_to_all x2 -> x1, starting transfers between devices: 24 us -> 17.6 us  [on_device(): lax.all_to_all(jnp.broadcast_to(wind_speeds[None], (wide, *wind_speeds.sh...]
    all_to_all x2 -> x1, waiting for transfers between devices: 18.4 us -> 12.5 us  [on_device(): lax.all_to_all(jnp.broadcast_to(wind_speeds[None], (wide, *wind_speeds.sh...]
    unnamed x7 -> x9, local copies, waits for them, and re-layouts: 1.14 us -> 0.19 us
  transfers between devices with their start and end apart: 3 -> 4, of which waited for: 3 -> 3; matrix products, arithmetic and copies ran while one was open for 1% -> 0% of each run, Pallas kernels for 1% -> 1%
where the time goes in v3:
time: 71 us; the launch traced here: 69.8 us
  starting transfers between devices  30.7 us (43%)
  waiting for transfers between devices  25.2 us (35%)
  Pallas kernels  11.2 us (16%)
  local copies, waits for them, and re-layouts  1.77 us (2%)
  other arithmetic  0.78 us (1%)
    all_to_all x1, starting transfers between devices, on_device(): lax.all_to_all(jnp.broadcast_to(wind_speeds[None], (wide, *wind_speeds.sh...  17.6 us
    all_to_all x1, waiting for transfers between devices, on_device(): lax.all_to_all(jnp.broadcast_to(wind_speeds[None], (wide, *wind_speeds.sh...  12.5 us
    all_to_all x1, waiting for transfers between devices, on_device(): cells = lax.all_to_all(moved.astype(SENT), 'wide', 0, 0, tiled=True)  12.2 us
    pallas_call x1, Pallas kernels, chemistry(): pl.pallas_call(chemistry_kernel, out_shape=jax.ShapeDtypeStruct((S, 1, co...  8.12 us
    all_to_all x1, starting transfers between devices, on_device(): cells = lax.all_to_all(moved.astype(SENT), 'wide', 0, 0, tiled=True)  5.74 us
    ppermute x1, starting transfers between devices, on_device(): lax.ppermute(rim(slice(RIM)), 'narrow', [(j, i) for i, j in down])  4.27 us
    ppermute x1, starting transfers between devices, on_device(): from_above = lax.ppermute(rim(slice(-RIM, None)), 'narrow', down)  3.12 us
    pallas_call x1, Pallas kernels, transport(): pl.pallas_call(transport_kernel, out_shape=jax.ShapeDtypeStruct(own.shape...  2.01 us
  transfers between devices with their start and end apart: 4, of which 3 were waited for; matrix products, arithmetic and copies ran while one was open for 0% of the time, Pallas kernels for 1%

profile of v3, /device:TPU:1, one launch (start us, length us, event | category | flops | bytes accessed | tf_op | source)
XLA Modules:
  0.0 69.8 jit_solution(3554822504578982865)
XLA Ops:
  0.0 0.0 copy-start.2
  0.0 1.4 %broadcast_in_dim.9 = bf16[64,2,2,1,256]{4,2,1,3,0:T(2,128)(2,1)} broadcast(bf16[2,2,256]{2,1,0:T(2,128)(2,1)} %bitcast.16), dimensions={1,2,4} | broadcast | bytes 133120 | tf_op jit(solution)/shard_map/broadcast_in_dim | solution.py:250
  1.5 17.6 %all-to-all-start = ((bf16[64,2,2,1,256]{4,2,1,3,0:T(2,128)(2,1)}), bf16[64,2,2,1,256]{4,2,1,3,0:T(2,128)(2,1)S(1)}, u32[]{:S(2)}, u32[]{:S(2)}) async-start(bf16[64,2,2,1,256]{4,2,1,3,0:T(2,128)(2,1)} %broadcast_in_dim.9), calls=%async_computation | async-start | bytes 262144 | tf_op jit(solution)/shard_map/all_to_all | solution.py:249
  19.1 0.0 copy-done.2
  19.1 0.2 copy.9
  19.3 12.5 %all-to-all-done = bf16[64,2,2,1,256]{4,2,1,3,0:T(2,128)(2,1)S(1)} async-done(((bf16[64,2,2,1,256]{4,2,1,3,0:T(2,128)(2,1)}), bf16[64,2,2,1,256]{4,2,1,3,0:T(2,128)(2,1)S(1)}, u32[]{:S(2)}, u32[]{:S(2)}) %all-to-all-start) | async-done | bytes 131104 | tf_op jit(solution)/shard_map/all_to_all | solution.py:249
  31.9 3.1 %collective-permute-start = (f32[4,8,256]{2,1,0:T(8,128)S(1)}, f32[4,8,256]{2,1,0:T(8,128)S(1)}, u32[]{:S(2)}, u32[]{:S(2)}) collective-permute-start(f32[4,8,256]{2,1,0:T(8,128)S(1)} %pad_maximum_fusion), channel_id=1, source_target_pairs={{0,1},{1,2},{2,3},{3,4},{4,5},{5,6},{6,7},{7,0},{8,9},{9,10},{10,1... | collective-permute-start | bytes 98312 | tf_op jit(solution)/shard_map/ppermute | solution.py:258
  35.0 0.0 copy-start.3
  35.1 4.3 %collective-permute-start.1 = (f32[4,8,256]{2,1,0:T(8,128)S(1)}, f32[4,8,256]{2,1,0:T(8,128)S(1)}, u32[]{:S(2)}, u32[]{:S(2)}) collective-permute-start(f32[4,8,256]{2,1,0:T(8,128)S(1)} %pad_maximum_fusion.1), channel_id=1, source_target_pairs={{1,0},{2,1},{3,2},{4,3},{5,4},{6,5},{7,6},{0,7},{9,8},{10,9},{11,1... | collective-permute-start | bytes 98312 | tf_op jit(solution)/shard_map/ppermute | solution.py:259
  39.3 0.4 maps.1
  39.8 0.0 copy-done.3
  39.8 0.1 reshape.15.winds_ref
  39.9 0.0 collective-permute-done.above_ref
  39.9 0.5 collective-permute-done.1.below_ref
  40.3 2.0 %transport.1 = f32[64,4,256]{2,1,0:T(4,128)S(1)} custom-call(f32[64,4,256]{2,1,0:T(4,128)S(1)} %bitcast.13, f32[4,8,256]{2,1,0:T(8,128)S(1)} %collective-permute-done.above_ref, f32[4,8,256]{2,1,0:T(8,128)S(1)} %collective-permute-done.1.below_ref, bf16[64,4,256]{2,1,0:T(4,128)(2,1)S(1)} %reshape.15.winds_ref, ...), custom_call_target="tpu_custom_call" | custom-call | flops 4000000000 | bytes 600000 | tf_op jit(solution)/shard_map/transport/pallas_call | solution.py:162
  42.4 0.7 %convert_element_type.22 = f16[64,4,256]{2,1,0:T(4,128)(2,1)} convert(f32[64,4,256]{2,1,0:T(4,128)S(1)} %transport.1) | non-fusion elementwise | flops 65536 | bytes 393216 | tf_op jit(solution)/shard_map/convert_element_type | solution.py:262
  43.1 0.0 copy-start
  43.1 0.0 copy-start.1
  43.1 5.7 %all-to-all-start.1 = ((f16[64,4,256]{2,1,0:T(4,128)(2,1)}), f16[64,4,256]{2,1,0:T(4,128)(2,1)S(1)}, u32[]{:S(2)}, u32[]{:S(2)}) async-start(f16[64,4,256]{2,1,0:T(4,128)(2,1)} %convert_element_type.22), calls=%async_computation.1 | async-start | bytes 262144 | tf_op jit(solution)/shard_map/all_to_all | solution.py:262
  48.8 0.0 copy-done
  48.8 0.0 copy-done.1
  48.8 0.6 tables.1
  49.5 12.2 %all-to-all-done.1 = f16[64,4,256]{2,1,0:T(4,128)(2,1)S(1)} async-done(((f16[64,4,256]{2,1,0:T(4,128)(2,1)}), f16[64,4,256]{2,1,0:T(4,128)(2,1)S(1)}, u32[]{:S(2)}, u32[]{:S(2)}) %all-to-all-start.1) | async-done | bytes 131104 | tf_op jit(solution)/shard_map/all_to_all | solution.py:262
  61.7 8.1 %chemistry.1 = f32[256,1,256]{2,1,0:T(1,128)} custom-call(f32[64,4,256]{2,1,0:T(4,128)S(1)} %convert_element_type.23.cells_ref, bf16[1536,256]{1,0:T(8,128)(2,1)S(1)} %get-tuple-element.14.pick_ref, bf16[256,768]{1,0:T(8,128)(2,1)S(1)} %get-tuple-element.15.net_ref, f32[768,128]{1,0:T(8,128)S(1)} %get-tuple-element.16.rate_ref), custom_call_target="tpu_custom_call" | custom-call | flops 4000000000 | bytes 2000000 | tf_op jit(solution)/shard_map/chemistry/pallas_call | solution.py:235
  (8 shorter events, 0.1 us)
Async XLA Ops:
  0.0 19.1 %copy-start.2 = (f32[4,64,256]{2,1,0:T(8,128)S(1)}, f32[4,64,256]{2,1,0:T(8,128)}, u32[]{:S(2)}) copy-start(f32[4,64,256]{2,1,0:T(8,128)} %param.5) | copy-start | bytes 786436
  1.5 30.4 %all-to-all-start = ((bf16[64,2,2,1,256]{4,2,1,3,0:T(2,128)(2,1)}), bf16[64,2,2,1,256]{4,2,1,3,0:T(2,128)(2,1)S(1)}, u32[]{:S(2)}, u32[]{:S(2)}) async-start(bf16[64,2,2,1,256]{4,2,1,3,0:T(2,128)(2,1)} %broadcast_in_dim.9), calls=%async_computation | async-start | bytes 262144 | tf_op jit(solution)/shard_map/all_to_all | solution.py:249
  31.9 8.0 %collective-permute-start = (f32[4,8,256]{2,1,0:T(8,128)S(1)}, f32[4,8,256]{2,1,0:T(8,128)S(1)}, u32[]{:S(2)}, u32[]{:S(2)}) collective-permute-start(f32[4,8,256]{2,1,0:T(8,128)S(1)} %pad_maximum_fusion), channel_id=1, source_target_pairs={{0,1},{1,2},{2,3},{3,4},{4,5},{5,6},{6,7},{7,0},{8,9},{9,10},{10,1... | collective-permute-start | bytes 98312 | tf_op jit(solution)/shard_map/ppermute | solution.py:258
  35.0 4.7 %copy-start.3 = (f32[768]{0:T(1024)S(1)}, f32[768]{0:T(1024)}, u32[]{:S(2)}) copy-start(f32[768]{0:T(1024)} %param.7) | copy-start | bytes 9220
  35.1 5.3 %collective-permute-start.1 = (f32[4,8,256]{2,1,0:T(8,128)S(1)}, f32[4,8,256]{2,1,0:T(8,128)S(1)}, u32[]{:S(2)}, u32[]{:S(2)}) collective-permute-start(f32[4,8,256]{2,1,0:T(8,128)S(1)} %pad_maximum_fusion.1), channel_id=1, source_target_pairs={{1,0},{2,1},{3,2},{4,3},{5,4},{6,5},{7,6},{0,7},{9,8},{10,9},{11,1... | collective-permute-start | bytes 98312 | tf_op jit(solution)/shard_map/ppermute | solution.py:259
  43.1 5.7 %copy-start = (s32[768,2]{0,1:T(2,128)S(1)}, s32[768,2]{0,1:T(2,128)}, u32[]{:S(2)}) copy-start(s32[768,2]{0,1:T(2,128)} %param.8) | copy-start | bytes 18436
  43.1 5.8 %copy-start.1 = (s32[768,2]{0,1:T(2,128)S(1)}, s32[768,2]{0,1:T(2,128)}, u32[]{:S(2)}) copy-start(s32[768,2]{0,1:T(2,128)} %param.9) | copy-start | bytes 18436
  43.1 18.6 %all-to-all-start.1 = ((f16[64,4,256]{2,1,0:T(4,128)(2,1)}), f16[64,4,256]{2,1,0:T(4,128)(2,1)S(1)}, u32[]{:S(2)}, u32[]{:S(2)}) async-start(f16[64,4,256]{2,1,0:T(4,128)(2,1)} %convert_element_type.22), calls=%async_computation.1 | async-start | bytes 262144 | tf_op jit(solution)/shard_map/all_to_all | solution.py:262

commit v4 on v3

--- a/solution.py
+++ b/solution.py
@@ -176,58 +176,68 @@
     )(own, above, below, winds, *constants)
 
 
-def tables_kernel(rates_ref, reactants_ref, products_ref, pick_ref, net_ref, rate_ref):
-    count = rates_ref.shape[-1]
+def tables_kernel(reactants_ref, products_ref, pick_ref, net_ref):
+    count = reactants_ref.shape[-1]
     ids = lax.broadcasted_iota(jnp.int32, (S, count), 0)
 
     def one_hot(ref, place):
         return jnp.where(ids == ref[place : place + 1, :], 1.0, 0.0)
 
     first, second = one_hot(reactants_ref, 0), one_hot(reactants_ref, 1)
-    pick_ref[0:count] = first.T.astype(jnp.bfloat16)
-    pick_ref[count:] = second.T.astype(jnp.bfloat16)
+    pick_ref[:, 0:count] = first.astype(jnp.bfloat16)
+    pick_ref[:, count:] = second.astype(jnp.bfloat16)
     net = one_hot(products_ref, 0) + one_hot(products_ref, 1) - first - second
-    net_ref[...] = net.astype(jnp.bfloat16)
-    rate_ref[...] = jnp.broadcast_to(rates_ref[...], (128, count)).T
+    net_ref[...] = net.T.astype(jnp.bfloat16)
 
 
 def tables(rate_constants, reactants, products):
     count = rate_constants.shape[0]
-    return pl.pallas_call(
+    made = pl.pallas_call(
         tables_kernel,
         out_shape=(
-            jax.ShapeDtypeStruct((2 * count, S), jnp.bfloat16),
-            jax.ShapeDtypeStruct((S, count), jnp.bfloat16),
-            jax.ShapeDtypeStruct((count, 128), jnp.float32),
+            jax.ShapeDtypeStruct((S, 2 * count), jnp.bfloat16),
+            jax.ShapeDtypeStruct((count, S), jnp.bfloat16),
         ),
-        in_specs=[pl.BlockSpec(memory_space=pltpu.VMEM)] * 3,
-        out_specs=(pl.BlockSpec(memory_space=pltpu.VMEM),) * 3,
+        in_specs=[pl.BlockSpec(memory_space=pltpu.VMEM)] * 2,
+        out_specs=(pl.BlockSpec(memory_space=pltpu.VMEM),) * 2,
         cost_estimate=pl.CostEstimate(flops=4_000_000_000, bytes_accessed=2_000_000, transcendentals=0),
         compiler_params=pltpu.CompilerParams(vmem_limit_bytes=16 << 20),
         name="tables",
-    )(rate_constants.reshape(1, count), reactants.T, products.T)
+    )(reactants.T, products.T)
+    return *made, rate_constants.reshape(1, count)
 
 
 def chemistry_kernel(cells_ref, pick_ref, net_ref, rate_ref, out_ref):
-    count = net_ref.shape[1]
+    count = net_ref.shape[0]
     chunk = 256
-    cells = cells_ref[...].reshape(S, cells_ref.shape[-1]).astype(jnp.float32)
-
-    def section(_, cells):
+    cells = cells_ref[...].reshape(S, cells_ref.shape[-1]).astype(jnp.float32).T
+
+    def picked(cells):
         high, low = two_terms(cells)
+        return [
+            matmul(high, pick_ref[:, at : at + chunk]) + matmul(low, pick_ref[:, at : at + chunk])
+            for at in range(0, 2 * count, chunk)
+        ]
+
+    def reacted(cells, found):
         change = jnp.zeros_like(cells)
-        for at in range(0, count, chunk):
-            here, there = slice(at, at + chunk), slice(count + at, count + at + chunk)
-            first = matmul(pick_ref[here], high) + matmul(pick_ref[here], low)
-            second = matmul(pick_ref[there], high) + matmul(pick_ref[there], low)
-            constant = rate_ref[here]
-            rate = jnp.concatenate([constant, constant], 1) * first * second
-            rate_high, rate_low = two_terms(rate)
-            change = change + matmul(net_ref[:, here], rate_high) + matmul(net_ref[:, here], rate_low)
+        for i, at in enumerate(range(0, count, chunk)):
+            here = slice(at, at + chunk)
+            pair = found[i] * found[i + count // chunk]
+            rate_high, rate_low = two_terms(rate_ref[:, here] * pair)
+            change = change + matmul(rate_high, net_ref[here]) + matmul(rate_low, net_ref[here])
         return cells + CHEM_STEP * change
 
-    cells = lax.fori_loop(0, SECTIONS, section, cells)
-    out_ref[...] = cells.reshape(out_ref.shape)
+    size = cells.shape[0] // 2
+    early, late = cells[:size], cells[size:]
+    found_late = picked(late)
+    for section in range(SECTIONS):
+        found_early = picked(early)
+        late = reacted(late, found_late)
+        early = reacted(early, found_early)
+        if section < SECTIONS - 1:
+            found_late = picked(late)
+    out_ref[...] = jnp.concatenate([early, late], 0).T.reshape(out_ref.shape)
 
 
 def chemistry(cells, pick, net, rate):

time: 71 us -> 68.5 us (0.965)
  Pallas kernels: 11.2 us -> 8.45 us
    pallas_call x1, Pallas kernels: 8.12 us -> 5.62 us  [chemistry(): pl.pallas_call(chemistry_kernel, out_shape=jax.ShapeDtypeStruct((S, 1, co...]
where the time goes in v4:
time: 68.5 us; the launch traced here: 67.3 us
  starting transfers between devices  30.7 us (45%)
  waiting for transfers between devices  25.4 us (37%)
  Pallas kernels  8.45 us (12%)
  local copies, waits for them, and re-layouts  1.77 us (3%)
  other arithmetic  0.78 us (1%)
    all_to_all x1, starting transfers between devices, on_device(): lax.all_to_all(jnp.broadcast_to(wind_speeds[None], (wide, *wind_speeds.sh...  17.6 us
    all_to_all x1, waiting for transfers between devices, on_device(): lax.all_to_all(jnp.broadcast_to(wind_speeds[None], (wide, *wind_speeds.sh...  12.5 us
    all_to_all x1, waiting for transfers between devices, on_device(): cells = lax.all_to_all(moved.astype(SENT), 'wide', 0, 0, tiled=True)  12.4 us
    all_to_all x1, starting transfers between devices, on_device(): cells = lax.all_to_all(moved.astype(SENT), 'wide', 0, 0, tiled=True)  5.74 us
    pallas_call x1, Pallas kernels, chemistry(): pl.pallas_call(chemistry_kernel, out_shape=jax.ShapeDtypeStruct((S, 1, co...  5.62 us
    ppermute x1, starting transfers between devices, on_device(): lax.ppermute(rim(slice(RIM)), 'narrow', [(j, i) for i, j in down])  4.27 us
    ppermute x1, starting transfers between devices, on_device(): from_above = lax.ppermute(rim(slice(-RIM, None)), 'narrow', down)  3.12 us
    pallas_call x1, Pallas kernels, transport(): pl.pallas_call(transport_kernel, out_shape=jax.ShapeDtypeStruct(own.shape...  2.01 us
  transfers between devices with their start and end apart: 4, of which 3 were waited for; matrix products, arithmetic and copies ran while one was open for 0% of the time, Pallas kernels for 1%

profile of v4, /device:TPU:1, one launch (start us, length us, event | category | flops | bytes accessed | tf_op | source)
XLA Modules:
  0.0 67.3 jit_solution(7035631910265730096)
XLA Ops:
  0.0 0.0 copy-start.2
  0.0 1.4 %broadcast_in_dim.9 = bf16[64,2,2,1,256]{4,2,1,3,0:T(2,128)(2,1)} broadcast(bf16[2,2,256]{2,1,0:T(2,128)(2,1)} %bitcast.16), dimensions={1,2,4} | broadcast | bytes 133120 | tf_op jit(solution)/shard_map/broadcast_in_dim | solution.py:260
  1.5 17.6 %all-to-all-start = ((bf16[64,2,2,1,256]{4,2,1,3,0:T(2,128)(2,1)}), bf16[64,2,2,1,256]{4,2,1,3,0:T(2,128)(2,1)S(1)}, u32[]{:S(2)}, u32[]{:S(2)}) async-start(bf16[64,2,2,1,256]{4,2,1,3,0:T(2,128)(2,1)} %broadcast_in_dim.9), calls=%async_computation | async-start | bytes 262144 | tf_op jit(solution)/shard_map/all_to_all | solution.py:259
  19.1 0.0 copy-done.2
  19.1 0.2 copy.9
  19.3 12.5 %all-to-all-done = bf16[64,2,2,1,256]{4,2,1,3,0:T(2,128)(2,1)S(1)} async-done(((bf16[64,2,2,1,256]{4,2,1,3,0:T(2,128)(2,1)}), bf16[64,2,2,1,256]{4,2,1,3,0:T(2,128)(2,1)S(1)}, u32[]{:S(2)}, u32[]{:S(2)}) %all-to-all-start) | async-done | bytes 131104 | tf_op jit(solution)/shard_map/all_to_all | solution.py:259
  31.9 3.1 %collective-permute-start = (f32[4,8,256]{2,1,0:T(8,128)S(1)}, f32[4,8,256]{2,1,0:T(8,128)S(1)}, u32[]{:S(2)}, u32[]{:S(2)}) collective-permute-start(f32[4,8,256]{2,1,0:T(8,128)S(1)} %pad_maximum_fusion), channel_id=1, source_target_pairs={{0,1},{1,2},{2,3},{3,4},{4,5},{5,6},{6,7},{7,0},{8,9},{9,10},{10,1... | collective-permute-start | bytes 98312 | tf_op jit(solution)/shard_map/ppermute | solution.py:268
  35.0 0.0 copy-start.3
  35.1 4.3 %collective-permute-start.1 = (f32[4,8,256]{2,1,0:T(8,128)S(1)}, f32[4,8,256]{2,1,0:T(8,128)S(1)}, u32[]{:S(2)}, u32[]{:S(2)}) collective-permute-start(f32[4,8,256]{2,1,0:T(8,128)S(1)} %pad_maximum_fusion.1), channel_id=1, source_target_pairs={{1,0},{2,1},{3,2},{4,3},{5,4},{6,5},{7,6},{0,7},{9,8},{10,9},{11,1... | collective-permute-start | bytes 98312 | tf_op jit(solution)/shard_map/ppermute | solution.py:269
  39.3 0.4 maps.1
  39.8 0.0 copy-done.3
  39.8 0.1 reshape.15.winds_ref
  39.9 0.0 collective-permute-done.above_ref
  39.9 0.5 collective-permute-done.1.below_ref
  40.3 2.0 %transport.1 = f32[64,4,256]{2,1,0:T(4,128)S(1)} custom-call(f32[64,4,256]{2,1,0:T(4,128)S(1)} %bitcast.13, f32[4,8,256]{2,1,0:T(8,128)S(1)} %collective-permute-done.above_ref, f32[4,8,256]{2,1,0:T(8,128)S(1)} %collective-permute-done.1.below_ref, bf16[64,4,256]{2,1,0:T(4,128)(2,1)S(1)} %reshape.15.winds_ref, ...), custom_call_target="tpu_custom_call" | custom-call | flops 4000000000 | bytes 600000 | tf_op jit(solution)/shard_map/transport/pallas_call | solution.py:162
  42.4 0.7 %convert_element_type.22 = f16[64,4,256]{2,1,0:T(4,128)(2,1)} convert(f32[64,4,256]{2,1,0:T(4,128)S(1)} %transport.1) | non-fusion elementwise | flops 65536 | bytes 393216 | tf_op jit(solution)/shard_map/convert_element_type | solution.py:272
  43.1 0.0 copy-start
  43.1 0.0 copy-start.1
  43.1 5.7 %all-to-all-start.1 = ((f16[64,4,256]{2,1,0:T(4,128)(2,1)}), f16[64,4,256]{2,1,0:T(4,128)(2,1)S(1)}, u32[]{:S(2)}, u32[]{:S(2)}) async-start(f16[64,4,256]{2,1,0:T(4,128)(2,1)} %convert_element_type.22), calls=%async_computation.1 | async-start | bytes 262144 | tf_op jit(solution)/shard_map/all_to_all | solution.py:272
  48.8 0.0 copy-done
  48.8 0.0 copy-done.1
  48.8 0.4 tables.1
  49.2 12.4 %all-to-all-done.1 = f16[64,4,256]{2,1,0:T(4,128)(2,1)S(1)} async-done(((f16[64,4,256]{2,1,0:T(4,128)(2,1)}), f16[64,4,256]{2,1,0:T(4,128)(2,1)S(1)}, u32[]{:S(2)}, u32[]{:S(2)}) %all-to-all-start.1) | async-done | bytes 131104 | tf_op jit(solution)/shard_map/all_to_all | solution.py:272
  61.7 5.6 %chemistry.1 = f32[256,1,256]{2,1,0:T(1,128)} custom-call(f32[64,4,256]{2,1,0:T(4,128)S(1)} %convert_element_type.23.cells_ref, bf16[256,1536]{1,0:T(8,128)(2,1)S(1)} %get-tuple-element.13.pick_ref, bf16[768,256]{1,0:T(8,128)(2,1)S(1)} %get-tuple-element.14.net_ref, f32[1,768]{1,0:T(1,128)S(1)} %reshape.16.rate_ref), custom_call_target="tpu_custom_call" | custom-call | flops 4000000000 | bytes 2000000 | tf_op jit(solution)/shard_map/chemistry/pallas_call | solution.py:245
  (8 shorter events, 0.1 us)
Async XLA Ops:
  0.0 19.1 %copy-start.2 = (f32[4,64,256]{2,1,0:T(8,128)S(1)}, f32[4,64,256]{2,1,0:T(8,128)}, u32[]{:S(2)}) copy-start(f32[4,64,256]{2,1,0:T(8,128)} %param.5) | copy-start | bytes 786436
  1.5 30.4 %all-to-all-start = ((bf16[64,2,2,1,256]{4,2,1,3,0:T(2,128)(2,1)}), bf16[64,2,2,1,256]{4,2,1,3,0:T(2,128)(2,1)S(1)}, u32[]{:S(2)}, u32[]{:S(2)}) async-start(bf16[64,2,2,1,256]{4,2,1,3,0:T(2,128)(2,1)} %broadcast_in_dim.9), calls=%async_computation | async-start | bytes 262144 | tf_op jit(solution)/shard_map/all_to_all | solution.py:259
  31.9 8.0 %collective-permute-start = (f32[4,8,256]{2,1,0:T(8,128)S(1)}, f32[4,8,256]{2,1,0:T(8,128)S(1)}, u32[]{:S(2)}, u32[]{:S(2)}) collective-permute-start(f32[4,8,256]{2,1,0:T(8,128)S(1)} %pad_maximum_fusion), channel_id=1, source_target_pairs={{0,1},{1,2},{2,3},{3,4},{4,5},{5,6},{6,7},{7,0},{8,9},{9,10},{10,1... | collective-permute-start | bytes 98312 | tf_op jit(solution)/shard_map/ppermute | solution.py:268
  35.0 4.7 %copy-start.3 = (f32[768]{0:T(1024)S(1)}, f32[768]{0:T(1024)}, u32[]{:S(2)}) copy-start(f32[768]{0:T(1024)} %param.7) | copy-start | bytes 9220
  35.1 5.3 %collective-permute-start.1 = (f32[4,8,256]{2,1,0:T(8,128)S(1)}, f32[4,8,256]{2,1,0:T(8,128)S(1)}, u32[]{:S(2)}, u32[]{:S(2)}) collective-permute-start(f32[4,8,256]{2,1,0:T(8,128)S(1)} %pad_maximum_fusion.1), channel_id=1, source_target_pairs={{1,0},{2,1},{3,2},{4,3},{5,4},{6,5},{7,6},{0,7},{9,8},{10,9},{11,1... | collective-permute-start | bytes 98312 | tf_op jit(solution)/shard_map/ppermute | solution.py:269
  43.1 5.7 %copy-start = (s32[768,2]{0,1:T(2,128)S(1)}, s32[768,2]{0,1:T(2,128)}, u32[]{:S(2)}) copy-start(s32[768,2]{0,1:T(2,128)} %param.8) | copy-start | bytes 18436
  43.1 5.8 %copy-start.1 = (s32[768,2]{0,1:T(2,128)S(1)}, s32[768,2]{0,1:T(2,128)}, u32[]{:S(2)}) copy-start(s32[768,2]{0,1:T(2,128)} %param.9) | copy-start | bytes 18436
  43.1 18.6 %all-to-all-start.1 = ((f16[64,4,256]{2,1,0:T(4,128)(2,1)}), f16[64,4,256]{2,1,0:T(4,128)(2,1)S(1)}, u32[]{:S(2)}, u32[]{:S(2)}) async-start(f16[64,4,256]{2,1,0:T(4,128)(2,1)} %convert_element_type.22), calls=%async_computation.1 | async-start | bytes 262144 | tf_op jit(solution)/shard_map/all_to_all | solution.py:272

commit v5 on v4

--- a/solution.py
+++ b/solution.py
@@ -1,11 +1,10 @@
-import functools
-
 import jax
 import jax.numpy as jnp
 from jax import lax
 from jax.experimental import pallas as pl
 from jax.experimental.pallas import tpu as pltpu
 from jax.sharding import PartitionSpec as P
+
 
 S = 256
 SUB = 2
@@ -41,17 +40,8 @@
     return [rows[i] - (fluxes[i] - fluxes[i - 1]) for i in range(2, count - 2)]
 
 
-def maps_kernel(pick_ref, shift_ref, face_ref, *, rows, groups, planes):
-    half = rows // 2
-    count = pick_ref.shape[1]
-    sources = pick_ref.shape[2]
+def maps_kernel(shift_ref, face_ref):
     lanes = shift_ref.shape[0]
-    at = lax.broadcasted_iota(jnp.int32, (count, sources), 0)
-    source = lax.broadcasted_iota(jnp.int32, (count, sources), 1)
-    start = (at // (2 * groups) + jnp.where(at % (2 * groups) < groups, 0, half)) * planes
-    for plane in range(planes):
-        weight = 1.0 if plane % 2 else 0.5
-        pick_ref[plane] = jnp.where(source == start + plane, weight, 0.0).astype(jnp.bfloat16)
     here = lax.broadcasted_iota(jnp.int32, (lanes, lanes), 0)
     there = lax.broadcasted_iota(jnp.int32, (lanes, lanes), 1)
     for i, step in enumerate((-2, -1, 1, 2)):
@@ -65,22 +55,15 @@
     face_ref[:, lanes:] = jnp.where(above, 0.5, 0.0).astype(jnp.bfloat16)
 
 
-def wind_depth(rows):
-    return pl.cdiv((rows + 2 * RIM) * SUB * 2, 128) * 128
-
-
-def maps(rows, groups, lanes):
-    planes = SUB * 2
-    count = (rows // 2 + 2 * RIM) * 2 * groups
+def maps(lanes):
     return pl.pallas_call(
-        functools.partial(maps_kernel, rows=rows, groups=groups, planes=planes),
+        maps_kernel,
         out_shape=(
-            jax.ShapeDtypeStruct((planes, count, wind_depth(rows)), jnp.bfloat16),
             jax.ShapeDtypeStruct((lanes, 4 * lanes), jnp.bfloat16),
             jax.ShapeDtypeStruct((lanes, 2 * lanes), jnp.bfloat16),
         ),
-        out_specs=(pl.BlockSpec(memory_space=pltpu.VMEM),) * 3,
-        cost_estimate=pl.CostEstimate(flops=2_000_000_000, bytes_accessed=2_000_000, transcendentals=0),
+        out_specs=(pl.BlockSpec(memory_space=pltpu.VMEM),) * 2,
+        cost_estimate=pl.CostEstimate(flops=2_000_000_000, bytes_accessed=1_000_000, transcendentals=0),
         compiler_params=pltpu.CompilerParams(vmem_limit_bytes=8 << 20),
         name="maps",
     )()
@@ -96,7 +79,7 @@
 
 
 def transport_kernel(
-    own_ref, above_ref, below_ref, winds_ref, pick_ref, shift_ref, face_ref, out_ref,
+    own_ref, above_ref, below_ref, winds_ref, shift_ref, face_ref, out_ref,
     ext_ref, wind_ref, moved_ref, speed_ref,
 ):
     rows, groups, lanes = own_ref.shape
@@ -111,30 +94,29 @@
     ext_ref[count - RIM : count, groups:] = below[:, :groups]
     rim, inner = RIM * planes, rows * planes
 
-    def wind_rows(cells):
-        return cells.astype(jnp.float32).reshape(-1, lanes).astype(jnp.bfloat16)
-
-    wind_ref[0:rim] = wind_rows(above[:, groups:])
-    wind_ref[rim : rim + inner] = wind_rows(winds_ref[...])
-    wind_ref[rim + inner : 2 * rim + inner] = wind_rows(below[:, groups:])
-    wind_ref[2 * rim + inner :] = jnp.zeros((wind_ref.shape[0] - 2 * rim - inner, lanes), jnp.bfloat16)
-    winds = wind_ref[...]
+    wind_ref[0:rim] = above[:, groups:].reshape(rim, lanes)
+    wind_ref[rim : rim + inner] = winds_ref[...].astype(jnp.float32).reshape(inner, lanes)
+    wind_ref[rim + inner :] = below[:, groups:].reshape(rim, lanes)
+    speed_ref[...] = matmul(wind_ref[...].astype(jnp.bfloat16), face_ref[...])
+    is_upper = lax.broadcasted_iota(jnp.int32, (tall, lanes), 0) < groups
+
+    def spread(ref, plane, at, columns):
+        here, there = (
+            jnp.broadcast_to(ref[row : row + 1, columns], (tall, lanes))
+            for row in (at * planes + plane, (at + half) * planes + plane)
+        )
+        return jnp.where(is_upper, here, there)
 
     field = [ext_ref[i] for i in range(count)]
     first = 0
     for substep in range(SUB):
-        low, high = first * tall, (first + len(field)) * tall
-        halves = matmul(pick_ref[2 * substep, low:high], winds)
-        speeds = [
-            halves[i * tall : (i + 1) * tall] + halves[(i + 1) * tall : (i + 2) * tall]
-            for i in range(len(field) - 1)
+        along = [
+            spread(wind_ref, 2 * substep, first + i, slice(0, lanes)) for i in range(len(field))
         ]
+        speeds = [0.5 * (along[i] + along[i + 1]) for i in range(len(field) - 1)]
         field = sweep_rows(field, speeds)
         first += 2
         size = len(field) * tall
-        low = first * tall
-        across = matmul(pick_ref[2 * substep + 1, low : low + size], winds).astype(jnp.bfloat16)
-        speed_ref[0:size] = matmul(across, face_ref[...])
         upper, lower = two_terms(jnp.concatenate(field, 0))
         moved_ref[0:size] = matmul(upper, shift_ref[...]) + matmul(lower, shift_ref[...])
         swept = []
@@ -145,8 +127,12 @@
             )
             jumps = [back1 - back2, row - back1, next1 - row, next2 - next1]
             slopes = [minmod(jumps[k], jumps[k + 1]) for k in range(3)]
-            low_flux = face_flux(back1, row, slopes[0], slopes[1], jumps[1], speed_ref[part, :lanes])
-            high_flux = face_flux(row, next1, slopes[1], slopes[2], jumps[2], speed_ref[part, lanes:])
+            low_speed, high_speed = (
+                spread(speed_ref, 2 * substep + 1, first + i, slice(k * lanes, (k + 1) * lanes))
+                for k in range(2)
+            )
+            low_flux = face_flux(back1, row, slopes[0], slopes[1], jumps[1], low_speed)
+            high_flux = face_flux(row, next1, slopes[1], slopes[2], jumps[2], high_speed)
             swept.append(row - (high_flux - low_flux))
         field = swept
     for i, row in enumerate(field):
@@ -154,21 +140,21 @@
         out_ref[half + i] = row[groups:].astype(out_ref.dtype)
 
 
-def transport(own, above, below, winds):
+def transport(own, above, below, winds, *constants):
     rows, groups, lanes = own.shape
     tall = 2 * groups
     size = (rows // 2 + 2 * RIM) * tall
-    constants = maps(rows, groups, lanes)
+    depth = (rows + 2 * RIM) * winds.shape[1]
     return pl.pallas_call(
         transport_kernel,
         out_shape=jax.ShapeDtypeStruct(own.shape, jnp.float32),
-        in_specs=[pl.BlockSpec(memory_space=pltpu.VMEM)] * 7,
+        in_specs=[pl.BlockSpec(memory_space=pltpu.VMEM)] * 6,
         out_specs=pl.BlockSpec(memory_space=pltpu.VMEM),
         scratch_shapes=[
             pltpu.VMEM((rows // 2 + 2 * RIM, tall, lanes), jnp.float32),
-            pltpu.VMEM((wind_depth(rows), lanes), jnp.bfloat16),
+            pltpu.VMEM((depth, lanes), jnp.float32),
             pltpu.VMEM((size, 4 * lanes), jnp.float32),
-            pltpu.VMEM((size, 2 * lanes), jnp.float32),
+            pltpu.VMEM((depth, 2 * lanes), jnp.float32),
         ],
         cost_estimate=pl.CostEstimate(flops=4_000_000_000, bytes_accessed=600_000, transcendentals=0),
         compiler_params=pltpu.CompilerParams(vmem_limit_bytes=16 << 20),
@@ -254,11 +240,12 @@
 
 
 def on_device(concentrations, wind_speeds, rate_constants, reactants, products):
-    groups, _, columns = concentrations.shape
+    _, _, columns = concentrations.shape
     wide, narrow = lax.axis_size("wide"), lax.axis_size("narrow")
     winds = lax.all_to_all(
         jnp.broadcast_to(wind_speeds[None], (wide, *wind_speeds.shape)), "wide", 0, 0, tiled=True
     ).reshape(wide, SUB * 2, columns)
+    moves = maps(columns)
     own = concentrations.swapaxes(0, 1)
 
     def rim(part):
@@ -268,7 +255,7 @@
     from_above = lax.ppermute(rim(slice(-RIM, None)), "narrow", down)
     from_below = lax.ppermute(rim(slice(RIM)), "narrow", [(j, i) for i, j in down])
     pick, net, rate = tables(rate_constants, reactants, products)
-    moved = transport(own, from_above, from_below, winds)
+    moved = transport(own, from_above, from_below, winds, *moves)
     cells = lax.all_to_all(moved.astype(SENT), "wide", 0, 0, tiled=True)
     return chemistry(cells.astype(jnp.float32), pick, net, rate)
 

time: 68.5 us -> 68.4 us (level)
  no operation moved by 1% of the time
where the time goes in v5:
time: 68.4 us; the launch traced here: 67.2 us
  starting transfers between devices  30.7 us (45%)
  waiting for transfers between devices  25.7 us (38%)
  Pallas kernels  8.1 us (12%)
  local copies, waits for them, and re-layouts  1.77 us (3%)
  other arithmetic  0.78 us (1%)
    all_to_all x1, starting transfers between devices, on_device(): lax.all_to_all(jnp.broadcast_to(wind_speeds[None], (wide, *wind_speeds.sh...  17.6 us
    all_to_all x1, waiting for transfers between devices, on_device(): lax.all_to_all(jnp.broadcast_to(wind_speeds[None], (wide, *wind_speeds.sh...  12.5 us
    all_to_all x1, waiting for transfers between devices, on_device(): cells = lax.all_to_all(moved.astype(SENT), 'wide', 0, 0, tiled=True)  12.4 us
    all_to_all x1, starting transfers between devices, on_device(): cells = lax.all_to_all(moved.astype(SENT), 'wide', 0, 0, tiled=True)  5.73 us
    pallas_call x1, Pallas kernels, chemistry(): pl.pallas_call(chemistry_kernel, out_shape=jax.ShapeDtypeStruct((S, 1, co...  5.62 us
    ppermute x1, starting transfers between devices, on_device(): lax.ppermute(rim(slice(RIM)), 'narrow', [(j, i) for i, j in down])  4.27 us
    ppermute x1, starting transfers between devices, on_device(): from_above = lax.ppermute(rim(slice(-RIM, None)), 'narrow', down)  3.12 us
    pallas_call x1, Pallas kernels, transport(): pl.pallas_call(transport_kernel, out_shape=jax.ShapeDtypeStruct(own.shape...  1.92 us
  transfers between devices with their start and end apart: 4, of which 3 were waited for; matrix products, arithmetic and copies ran while one was open for 0% of the time, Pallas kernels for 1%

profile of v5, /device:TPU:1, one launch (start us, length us, event | category | flops | bytes accessed | tf_op | source)
XLA Modules:
  0.0 67.2 jit_solution(14141139648009007299)
XLA Ops:
  0.0 0.0 copy-start.2
  0.0 1.4 %broadcast_in_dim.9 = bf16[64,2,2,1,256]{4,2,1,3,0:T(2,128)(2,1)} broadcast(bf16[2,2,256]{2,1,0:T(2,128)(2,1)} %bitcast.16), dimensions={1,2,4} | broadcast | bytes 133120 | tf_op jit(solution)/shard_map/broadcast_in_dim | solution.py:246
  1.5 17.6 %all-to-all-start = ((bf16[64,2,2,1,256]{4,2,1,3,0:T(2,128)(2,1)}), bf16[64,2,2,1,256]{4,2,1,3,0:T(2,128)(2,1)S(1)}, u32[]{:S(2)}, u32[]{:S(2)}) async-start(bf16[64,2,2,1,256]{4,2,1,3,0:T(2,128)(2,1)} %broadcast_in_dim.9), calls=%async_computation | async-start | bytes 262144 | tf_op jit(solution)/shard_map/all_to_all | solution.py:245
  19.1 0.0 copy-done.2
  19.1 0.2 copy.9
  19.3 12.5 %all-to-all-done = bf16[64,2,2,1,256]{4,2,1,3,0:T(2,128)(2,1)S(1)} async-done(((bf16[64,2,2,1,256]{4,2,1,3,0:T(2,128)(2,1)}), bf16[64,2,2,1,256]{4,2,1,3,0:T(2,128)(2,1)S(1)}, u32[]{:S(2)}, u32[]{:S(2)}) %all-to-all-start) | async-done | bytes 131104 | tf_op jit(solution)/shard_map/all_to_all | solution.py:245
  31.9 3.1 %collective-permute-start = (f32[4,8,256]{2,1,0:T(8,128)S(1)}, f32[4,8,256]{2,1,0:T(8,128)S(1)}, u32[]{:S(2)}, u32[]{:S(2)}) collective-permute-start(f32[4,8,256]{2,1,0:T(8,128)S(1)} %pad_maximum_fusion), channel_id=1, source_target_pairs={{0,1},{1,2},{2,3},{3,4},{4,5},{5,6},{6,7},{7,0},{8,9},{9,10},{10,1... | collective-permute-start | bytes 98312 | tf_op jit(solution)/shard_map/ppermute | solution.py:255
  35.0 0.0 copy-start.3
  35.1 4.3 %collective-permute-start.1 = (f32[4,8,256]{2,1,0:T(8,128)S(1)}, f32[4,8,256]{2,1,0:T(8,128)S(1)}, u32[]{:S(2)}, u32[]{:S(2)}) collective-permute-start(f32[4,8,256]{2,1,0:T(8,128)S(1)} %pad_maximum_fusion.1), channel_id=1, source_target_pairs={{1,0},{2,1},{3,2},{4,3},{5,4},{6,5},{7,6},{0,7},{9,8},{10,9},{11,1... | collective-permute-start | bytes 98312 | tf_op jit(solution)/shard_map/ppermute | solution.py:256
  39.3 0.2 maps.1
  39.5 0.0 copy-done.3
  39.5 0.1 reshape.15.winds_ref
  39.6 0.0 collective-permute-done.above_ref
  39.6 0.7 %collective-permute-done.1.below_ref = f32[4,8,256]{2,1,0:T(8,128)S(1)} collective-permute-done((f32[4,8,256]{2,1,0:T(8,128)S(1)}, f32[4,8,256]{2,1,0:T(8,128)S(1)}, u32[]{:S(2)}, u32[]{:S(2)}) %collective-permute-start.1) | collective-permute-done | bytes 32800 | tf_op jit(solution)/shard_map/ppermute | solution.py:256
  40.3 1.9 %transport.1 = f32[64,4,256]{2,1,0:T(4,128)S(1)} custom-call(f32[64,4,256]{2,1,0:T(4,128)S(1)} %bitcast.13, f32[4,8,256]{2,1,0:T(8,128)S(1)} %collective-permute-done.above_ref, f32[4,8,256]{2,1,0:T(8,128)S(1)} %collective-permute-done.1.below_ref, bf16[64,4,256]{2,1,0:T(4,128)(2,1)S(1)} %reshape.15.winds_ref, ...), custom_call_target="tpu_custom_call" | custom-call | flops 4000000000 | bytes 600000 | tf_op jit(solution)/shard_map/transport/pallas_call | solution.py:148
  42.3 0.7 %convert_element_type.22 = f16[64,4,256]{2,1,0:T(4,128)(2,1)} convert(f32[64,4,256]{2,1,0:T(4,128)S(1)} %transport.1) | non-fusion elementwise | flops 65536 | bytes 393216 | tf_op jit(solution)/shard_map/convert_element_type | solution.py:259
  43.0 0.0 copy-start
  43.0 0.0 copy-start.1
  43.0 5.7 %all-to-all-start.1 = ((f16[64,4,256]{2,1,0:T(4,128)(2,1)}), f16[64,4,256]{2,1,0:T(4,128)(2,1)S(1)}, u32[]{:S(2)}, u32[]{:S(2)}) async-start(f16[64,4,256]{2,1,0:T(4,128)(2,1)} %convert_element_type.22), calls=%async_computation.1 | async-start | bytes 262144 | tf_op jit(solution)/shard_map/all_to_all | solution.py:259
  48.7 0.0 copy-done
  48.7 0.0 copy-done.1
  48.7 0.4 tables.1
  49.1 12.4 %all-to-all-done.1 = f16[64,4,256]{2,1,0:T(4,128)(2,1)S(1)} async-done(((f16[64,4,256]{2,1,0:T(4,128)(2,1)}), f16[64,4,256]{2,1,0:T(4,128)(2,1)S(1)}, u32[]{:S(2)}, u32[]{:S(2)}) %all-to-all-start.1) | async-done | bytes 131104 | tf_op jit(solution)/shard_map/all_to_all | solution.py:259
  61.6 5.6 %chemistry.1 = f32[256,1,256]{2,1,0:T(1,128)} custom-call(f32[64,4,256]{2,1,0:T(4,128)S(1)} %convert_element_type.23.cells_ref, bf16[256,1536]{1,0:T(8,128)(2,1)S(1)} %get-tuple-element.11.pick_ref, bf16[768,256]{1,0:T(8,128)(2,1)S(1)} %get-tuple-element.12.net_ref, f32[1,768]{1,0:T(1,128)S(1)} %reshape.16.rate_ref), custom_call_target="tpu_custom_call" | custom-call | flops 4000000000 | bytes 2000000 | tf_op jit(solution)/shard_map/chemistry/pallas_call | solution.py:231
  (8 shorter events, 0.1 us)
Async XLA Ops:
  0.0 19.1 %copy-start.2 = (f32[4,64,256]{2,1,0:T(8,128)S(1)}, f32[4,64,256]{2,1,0:T(8,128)}, u32[]{:S(2)}) copy-start(f32[4,64,256]{2,1,0:T(8,128)} %param.5) | copy-start | bytes 786436
  1.5 30.4 %all-to-all-start = ((bf16[64,2,2,1,256]{4,2,1,3,0:T(2,128)(2,1)}), bf16[64,2,2,1,256]{4,2,1,3,0:T(2,128)(2,1)S(1)}, u32[]{:S(2)}, u32[]{:S(2)}) async-start(bf16[64,2,2,1,256]{4,2,1,3,0:T(2,128)(2,1)} %broadcast_in_dim.9), calls=%async_computation | async-start | bytes 262144 | tf_op jit(solution)/shard_map/all_to_all | solution.py:245
  31.9 7.7 %collective-permute-start = (f32[4,8,256]{2,1,0:T(8,128)S(1)}, f32[4,8,256]{2,1,0:T(8,128)S(1)}, u32[]{:S(2)}, u32[]{:S(2)}) collective-permute-start(f32[4,8,256]{2,1,0:T(8,128)S(1)} %pad_maximum_fusion), channel_id=1, source_target_pairs={{0,1},{1,2},{2,3},{3,4},{4,5},{5,6},{6,7},{7,0},{8,9},{9,10},{10,1... | collective-permute-start | bytes 98312 | tf_op jit(solution)/shard_map/ppermute | solution.py:255
  35.0 4.5 %copy-start.3 = (f32[768]{0:T(1024)S(1)}, f32[768]{0:T(1024)}, u32[]{:S(2)}) copy-start(f32[768]{0:T(1024)} %param.7) | copy-start | bytes 9220
  35.1 5.3 %collective-permute-start.1 = (f32[4,8,256]{2,1,0:T(8,128)S(1)}, f32[4,8,256]{2,1,0:T(8,128)S(1)}, u32[]{:S(2)}, u32[]{:S(2)}) collective-permute-start(f32[4,8,256]{2,1,0:T(8,128)S(1)} %pad_maximum_fusion.1), channel_id=1, source_target_pairs={{1,0},{2,1},{3,2},{4,3},{5,4},{6,5},{7,6},{0,7},{9,8},{10,9},{11,1... | collective-permute-start | bytes 98312 | tf_op jit(solution)/shard_map/ppermute | solution.py:256
  43.0 5.7 %copy-start = (s32[768,2]{0,1:T(2,128)S(1)}, s32[768,2]{0,1:T(2,128)}, u32[]{:S(2)}) copy-start(s32[768,2]{0,1:T(2,128)} %param.8) | copy-start | bytes 18436
  43.0 5.7 %copy-start.1 = (s32[768,2]{0,1:T(2,128)S(1)}, s32[768,2]{0,1:T(2,128)}, u32[]{:S(2)}) copy-start(s32[768,2]{0,1:T(2,128)} %param.9) | copy-start | bytes 18436
  43.0 18.6 %all-to-all-start.1 = ((f16[64,4,256]{2,1,0:T(4,128)(2,1)}), f16[64,4,256]{2,1,0:T(4,128)(2,1)S(1)}, u32[]{:S(2)}, u32[]{:S(2)}) async-start(f16[64,4,256]{2,1,0:T(4,128)(2,1)} %convert_element_type.22), calls=%async_computation.1 | async-start | bytes 262144 | tf_op jit(solution)/shard_map/all_to_all | solution.py:259

commit v6 on v5

--- a/solution.py
+++ b/solution.py
@@ -78,32 +78,16 @@
     return high, (x - high.astype(jnp.float32)).astype(jnp.bfloat16)
 
 
-def transport_kernel(
-    own_ref, above_ref, below_ref, winds_ref, shift_ref, face_ref, out_ref,
-    ext_ref, wind_ref, moved_ref, speed_ref,
-):
-    rows, groups, lanes = own_ref.shape
-    planes = winds_ref.shape[1]
-    tall = 2 * groups
-    half = rows // 2
-    count = half + 2 * RIM
-    above, below = above_ref[...], below_ref[...]
-    ext_ref[0:RIM, 0:groups] = above[:, :groups]
-    ext_ref[RIM:count, 0:groups] = own_ref[0 : half + RIM]
-    ext_ref[0 : count - RIM, groups:] = own_ref[half - RIM : rows]
-    ext_ref[count - RIM : count, groups:] = below[:, :groups]
-    rim, inner = RIM * planes, rows * planes
-
-    wind_ref[0:rim] = above[:, groups:].reshape(rim, lanes)
-    wind_ref[rim : rim + inner] = winds_ref[...].astype(jnp.float32).reshape(inner, lanes)
-    wind_ref[rim + inner :] = below[:, groups:].reshape(rim, lanes)
+def swept_rows(ext_ref, wind_ref, moved_ref, speed_ref, shift_ref, face_ref, planes):
+    count, tall, lanes = ext_ref.shape
+    apart = wind_ref.shape[0] // planes - count
     speed_ref[...] = matmul(wind_ref[...].astype(jnp.bfloat16), face_ref[...])
-    is_upper = lax.broadcasted_iota(jnp.int32, (tall, lanes), 0) < groups
+    is_upper = lax.broadcasted_iota(jnp.int32, (tall, lanes), 0) < tall // 2
 
     def spread(ref, plane, at, columns):
         here, there = (
             jnp.broadcast_to(ref[row : row + 1, columns], (tall, lanes))
-            for row in (at * planes + plane, (at + half) * planes + plane)
+            for row in (at * planes + plane, (at + apart) * planes + plane)
         )
         return jnp.where(is_upper, here, there)
 
@@ -135,31 +119,65 @@
             high_flux = face_flux(row, next1, slopes[1], slopes[2], jumps[2], high_speed)
             swept.append(row - (high_flux - low_flux))
         field = swept
+    return field
+
+
+def put(field, out_ref):
+    groups = out_ref.shape[1]
     for i, row in enumerate(field):
-        out_ref[i] = row[0:groups].astype(out_ref.dtype)
-        out_ref[half + i] = row[groups:].astype(out_ref.dtype)
-
-
-def transport(own, above, below, winds, *constants):
-    rows, groups, lanes = own.shape
-    tall = 2 * groups
-    size = (rows // 2 + 2 * RIM) * tall
-    depth = (rows + 2 * RIM) * winds.shape[1]
+        out_ref[i] = row[0:groups]
+        out_ref[len(field) + i] = row[groups:]
+
+
+def inner_kernel(own_ref, winds_ref, shift_ref, face_ref, out_ref, ext_ref, wind_ref, moved_ref, speed_ref):
+    rows, groups, lanes = own_ref.shape
+    planes = winds_ref.shape[1]
+    count = ext_ref.shape[0]
+    ext_ref[:, 0:groups] = own_ref[0:count]
+    ext_ref[:, groups:] = own_ref[rows - count : rows]
+    wind_ref[...] = winds_ref[...].astype(jnp.float32).reshape(rows * planes, lanes)
+    put(swept_rows(ext_ref, wind_ref, moved_ref, speed_ref, shift_ref, face_ref, planes), out_ref)
+
+
+def outer_kernel(
+    own_ref, winds_ref, above_ref, below_ref, shift_ref, face_ref, out_ref,
+    ext_ref, wind_ref, moved_ref, speed_ref,
+):
+    rows, groups, lanes = own_ref.shape
+    planes = winds_ref.shape[1]
+    near = 2 * RIM
+    above, below = above_ref[...], below_ref[...]
+    ext_ref[0:RIM, 0:groups] = above[:, :groups]
+    ext_ref[RIM:, 0:groups] = own_ref[0:near]
+    ext_ref[0:near, groups:] = own_ref[rows - near : rows]
+    ext_ref[near:, groups:] = below[:, :groups]
+    rim, block = RIM * planes, near * planes
+    wind_ref[0:rim] = above[:, groups:].reshape(rim, lanes)
+    wind_ref[rim : rim + block] = winds_ref[0:near].astype(jnp.float32).reshape(block, lanes)
+    wind_ref[rim + block : rim + 2 * block] = (
+        winds_ref[rows - near : rows].astype(jnp.float32).reshape(block, lanes)
+    )
+    wind_ref[rim + 2 * block :] = below[:, groups:].reshape(rim, lanes)
+    put(swept_rows(ext_ref, wind_ref, moved_ref, speed_ref, shift_ref, face_ref, planes), out_ref)
+
+
+def sweep_call(kernel, count, depth, flops, own, winds, *others):
+    _, groups, lanes = own.shape
+    tall, planes = 2 * groups, winds.shape[1]
     return pl.pallas_call(
-        transport_kernel,
-        out_shape=jax.ShapeDtypeStruct(own.shape, jnp.float32),
-        in_specs=[pl.BlockSpec(memory_space=pltpu.VMEM)] * 6,
+        kernel,
+        out_shape=jax.ShapeDtypeStruct((2 * (count - 2 * RIM), groups, lanes), jnp.float32),
+        in_specs=[pl.BlockSpec(memory_space=pltpu.VMEM)] * (2 + len(others)),
         out_specs=pl.BlockSpec(memory_space=pltpu.VMEM),
         scratch_shapes=[
-            pltpu.VMEM((rows // 2 + 2 * RIM, tall, lanes), jnp.float32),
-            pltpu.VMEM((depth, lanes), jnp.float32),
-            pltpu.VMEM((size, 4 * lanes), jnp.float32),
-            pltpu.VMEM((depth, 2 * lanes), jnp.float32),
+            pltpu.VMEM((count, tall, lanes), jnp.float32),
+            pltpu.VMEM((depth * planes, lanes), jnp.float32),
+            pltpu.VMEM((count * tall, 4 * lanes), jnp.float32),
+            pltpu.VMEM((depth * planes, 2 * lanes), jnp.float32),
         ],
-        cost_estimate=pl.CostEstimate(flops=4_000_000_000, bytes_accessed=600_000, transcendentals=0),
+        cost_estimate=pl.CostEstimate(flops=flops, bytes_accessed=600_000, transcendentals=0),
         compiler_params=pltpu.CompilerParams(vmem_limit_bytes=16 << 20),
-        name="transport",
-    )(own, above, below, winds, *constants)
+    )(own, winds, *others)
 
 
 def tables_kernel(reactants_ref, products_ref, pick_ref, net_ref):
@@ -255,7 +273,13 @@
     from_above = lax.ppermute(rim(slice(-RIM, None)), "narrow", down)
     from_below = lax.ppermute(rim(slice(RIM)), "narrow", [(j, i) for i, j in down])
     pick, net, rate = tables(rate_constants, reactants, products)
-    moved = transport(own, from_above, from_below, winds, *moves)
+    rows = own.shape[0]
+    inner = sweep_call(inner_kernel, rows // 2 + RIM, rows, 4_000_000_000, own, winds, *moves)
+    outer = sweep_call(
+        outer_kernel, 3 * RIM, 6 * RIM, 1_000_000_000, own, winds, from_above, from_below,
+        *moves,
+    )
+    moved = jnp.concatenate([outer[:RIM], inner, outer[RIM:]], 0)
     cells = lax.all_to_all(moved.astype(SENT), "wide", 0, 0, tiled=True)
     return chemistry(cells.astype(jnp.float32), pick, net, rate)
 

time: 68.4 us -> 67.3 us (0.984)
  waiting for transfers between devices: 25.7 us -> 24 us
  local copies, waits for them, and re-layouts: 1.77 us -> 2.52 us
    all_to_all x1, waiting for transfers between devices: 12.5 us -> 11.6 us  [on_device(): lax.all_to_all(jnp.broadcast_to(wind_speeds[None], (wide, *wind_speeds.sh...]
    unnamed x9, local copies, waits for them, and re-layouts: 0.19 us -> 0.97 us
    concatenate x0 -> x1, other arithmetic: none -> 0.76 us  [on_device(): moved = jnp.concatenate([outer[:RIM], inner, outer[RIM:]], 0)]
    ppermute x1, waiting for transfers between devices: 0.73 us -> 0.01 us  [on_device(): lax.ppermute(rim(slice(RIM)), 'narrow', [(j, i) for i, j in down])]
    convert_element_type x1 -> x0, other arithmetic: 0.7 us -> none  [on_device(): cells = lax.all_to_all(moved.astype(SENT), 'wide', 0, 0, tiled=True)]
    pallas_call x1 -> x2, Pallas kernels: 1.92 us -> 2.46 us  [sweep_call(): pl.pallas_call(kernel, out_shape=jax.ShapeDtypeStruct((2 * (count - 2 * R...]
  transfers between devices with their start and end apart: 4 -> 4, of which waited for: 3 -> 2; matrix products, arithmetic and copies ran while one was open for 0% -> 0% of each run, Pallas kernels for 1% -> 3%
where the time goes in v6:
time: 67.3 us; the launch traced here: 66.4 us
  starting transfers between devices  30.2 us (45%)
  waiting for transfers between devices  24 us (36%)
  Pallas kernels  8.64 us (13%)
  local copies, waits for them, and re-layouts  2.52 us (4%)
  other arithmetic  0.9 us (1%)
    all_to_all x1, starting transfers between devices, on_device(): lax.all_to_all(jnp.broadcast_to(wind_speeds[None], (wide, *wind_speeds.sh...  17.6 us
    all_to_all x1, waiting for transfers between devices, on_device(): cells = lax.all_to_all(moved.astype(SENT), 'wide', 0, 0, tiled=True)  12.4 us
    all_to_all x1, waiting for transfers between devices, on_device(): lax.all_to_all(jnp.broadcast_to(wind_speeds[None], (wide, *wind_speeds.sh...  11.6 us
    pallas_call x1, Pallas kernels, chemistry(): pl.pallas_call(chemistry_kernel, out_shape=jax.ShapeDtypeStruct((S, 1, co...  5.62 us
    all_to_all x1, starting transfers between devices, on_device(): cells = lax.all_to_all(moved.astype(SENT), 'wide', 0, 0, tiled=True)  5.15 us
    ppermute x1, starting transfers between devices, on_device(): lax.ppermute(rim(slice(RIM)), 'narrow', [(j, i) for i, j in down])  4.27 us
    ppermute x1, starting transfers between devices, on_device(): from_above = lax.ppermute(rim(slice(-RIM, None)), 'narrow', down)  3.12 us
    pallas_call x2, Pallas kernels, sweep_call(): pl.pallas_call(kernel, out_shape=jax.ShapeDtypeStruct((2 * (count - 2 * R...  2.46 us
  transfers between devices with their start and end apart: 4, of which 2 were waited for; matrix products, arithmetic and copies ran while one was open for 0% of the time, Pallas kernels for 3%

profile of v6, /device:TPU:1, one launch (start us, length us, event | category | flops | bytes accessed | tf_op | source)
XLA Modules:
  0.0 66.4 jit_solution(956975577120220527)
XLA Ops:
  0.0 1.4 %broadcast_in_dim.9 = bf16[64,2,2,1,256]{4,2,1,3,0:T(2,128)(2,1)} broadcast(bf16[2,2,256]{2,1,0:T(2,128)(2,1)} %bitcast.17), dimensions={1,2,4} | broadcast | bytes 133120 | tf_op jit(solution)/shard_map/broadcast_in_dim | solution.py:264
  1.4 17.6 %all-to-all-start = ((bf16[64,2,2,1,256]{4,2,1,3,0:T(2,128)(2,1)}), bf16[64,2,2,1,256]{4,2,1,3,0:T(2,128)(2,1)S(1)}, u32[]{:S(2)}, u32[]{:S(2)}) async-start(bf16[64,2,2,1,256]{4,2,1,3,0:T(2,128)(2,1)} %broadcast_in_dim.9), calls=%async_computation | async-start | bytes 262144 | tf_op jit(solution)/shard_map/all_to_all | solution.py:263
  19.0 0.0 copy-start.3
  19.0 0.0 copy-start.2
  19.1 0.2 maps.1
  19.2 0.5 copy-done.3
  19.7 0.3 copy-done.2
  20.0 0.2 copy.9
  20.2 11.6 %all-to-all-done = bf16[64,2,2,1,256]{4,2,1,3,0:T(2,128)(2,1)S(1)} async-done(((bf16[64,2,2,1,256]{4,2,1,3,0:T(2,128)(2,1)}), bf16[64,2,2,1,256]{4,2,1,3,0:T(2,128)(2,1)S(1)}, u32[]{:S(2)}, u32[]{:S(2)}) %all-to-all-start) | async-done | bytes 131104 | tf_op jit(solution)/shard_map/all_to_all | solution.py:263
  31.9 3.1 %collective-permute-start = (f32[4,8,256]{2,1,0:T(8,128)S(1)}, f32[4,8,256]{2,1,0:T(8,128)S(1)}, u32[]{:S(2)}, u32[]{:S(2)}) collective-permute-start(f32[4,8,256]{2,1,0:T(8,128)S(1)} %pad_maximum_fusion.1), channel_id=1, source_target_pairs={{0,1},{1,2},{2,3},{3,4},{4,5},{5,6},{6,7},{7,0},{8,9},{9,10},{10,1... | collective-permute-start | bytes 98312 | tf_op jit(solution)/shard_map/ppermute | solution.py:273
  35.0 4.3 %collective-permute-start.1 = (f32[4,8,256]{2,1,0:T(8,128)S(1)}, f32[4,8,256]{2,1,0:T(8,128)S(1)}, u32[]{:S(2)}, u32[]{:S(2)}) collective-permute-start(f32[4,8,256]{2,1,0:T(8,128)S(1)} %pad_maximum_fusion.2), channel_id=1, source_target_pairs={{1,0},{2,1},{3,2},{4,3},{5,4},{6,5},{7,6},{0,7},{9,8},{10,9},{11,1... | collective-permute-start | bytes 98312 | tf_op jit(solution)/shard_map/ppermute | solution.py:274
  39.3 0.1 reshape.15.winds_ref
  39.4 1.7 %shard_map.56 = f32[56,4,256]{2,1,0:T(4,128)S(1)} custom-call(f32[64,4,256]{2,1,0:T(4,128)S(1)} %bitcast.13, bf16[64,4,256]{2,1,0:T(4,128)(2,1)S(1)} %reshape.15.winds_ref, bf16[256,1024]{1,0:T(8,128)(2,1)S(1)} %get-tuple-element.9.shift_ref, bf16[256,512]{1,0:T(8,128)(2,1)S(1)} %get-tuple-element.10.face_ref), custom_call_target="tpu_custom_call" | custom-call | flops 4000000000 | bytes 600000 | tf_op jit(solution)/shard_map/pallas_call | solution.py:167
  41.1 0.0 collective-permute-done.above_ref
  41.1 0.0 collective-permute-done.1.below_ref
  41.1 0.8 %shard_map.55 = f32[8,4,256]{2,1,0:T(4,128)S(1)} custom-call(f32[64,4,256]{2,1,0:T(4,128)S(1)} %bitcast.14, bf16[64,4,256]{2,1,0:T(4,128)(2,1)S(1)} %reshape.15.winds_ref, f32[4,8,256]{2,1,0:T(8,128)S(1)} %collective-permute-done.above_ref, f32[4,8,256]{2,1,0:T(8,128)S(1)} %collective-permute-done.1.below_ref, ...), custom_call_target="tpu_custom_call" | custom-call | flops 1000000000 | bytes 600000 | tf_op jit(solution)/shard_map/pallas_call | solution.py:167
  41.9 0.8 %pad_maximum_fusion = f16[64,4,256]{2,1,0:T(4,128)(2,1)} fusion(f16[4,4,256]{2,1,0:T(4,128)(2,1)S(1)} %get-tuple-element.18, f16[56,4,256]{2,1,0:T(4,128)(2,1)S(1)} %convert.12, f16[4,4,256]{2,1,0:T(4,128)(2,1)S(1)} %get-tuple-element.17), kind=kLoop, calls=%fused_computation.1 | loop fusion | flops 131072 | bytes 262144 | tf_op jit(solution)/shard_map/concatenate | solution.py:282
  42.7 0.0 copy-start
  42.7 0.0 copy-start.1
  42.7 5.2 %all-to-all-start.1 = ((f16[64,4,256]{2,1,0:T(4,128)(2,1)}), f16[64,4,256]{2,1,0:T(4,128)(2,1)S(1)}, u32[]{:S(2)}, u32[]{:S(2)}) async-start(f16[64,4,256]{2,1,0:T(4,128)(2,1)} %pad_maximum_fusion), calls=%async_computation.1 | async-start | bytes 262144 | tf_op jit(solution)/shard_map/all_to_all | solution.py:283
  47.9 0.0 copy-done
  47.9 0.0 copy-done.1
  47.9 0.4 tables.1
  48.3 12.4 %all-to-all-done.1 = f16[64,4,256]{2,1,0:T(4,128)(2,1)S(1)} async-done(((f16[64,4,256]{2,1,0:T(4,128)(2,1)}), f16[64,4,256]{2,1,0:T(4,128)(2,1)S(1)}, u32[]{:S(2)}, u32[]{:S(2)}) %all-to-all-start.1) | async-done | bytes 131104 | tf_op jit(solution)/shard_map/all_to_all | solution.py:283
  60.8 5.6 %chemistry.1 = f32[256,1,256]{2,1,0:T(1,128)} custom-call(f32[64,4,256]{2,1,0:T(4,128)S(1)} %convert_element_type.20.cells_ref, bf16[256,1536]{1,0:T(8,128)(2,1)S(1)} %get-tuple-element.11.pick_ref, bf16[768,256]{1,0:T(8,128)(2,1)S(1)} %get-tuple-element.12.net_ref, f32[1,768]{1,0:T(1,128)S(1)} %reshape.16.rate_ref), custom_call_target="tpu_custom_call" | custom-call | flops 4000000000 | bytes 2000000 | tf_op jit(solution)/shard_map/chemistry/pallas_call | solution.py:249
  (11 shorter events, 0.2 us)
Async XLA Ops:
  1.4 30.4 %all-to-all-start = ((bf16[64,2,2,1,256]{4,2,1,3,0:T(2,128)(2,1)}), bf16[64,2,2,1,256]{4,2,1,3,0:T(2,128)(2,1)S(1)}, u32[]{:S(2)}, u32[]{:S(2)}) async-start(bf16[64,2,2,1,256]{4,2,1,3,0:T(2,128)(2,1)} %broadcast_in_dim.9), calls=%async_computation | async-start | bytes 262144 | tf_op jit(solution)/shard_map/all_to_all | solution.py:263
  19.0 0.7 %copy-start.3 = (f32[768]{0:T(1024)S(1)}, f32[768]{0:T(1024)}, u32[]{:S(2)}) copy-start(f32[768]{0:T(1024)} %param.7) | copy-start | bytes 9220
  19.0 1.0 %copy-start.2 = (f32[4,64,256]{2,1,0:T(8,128)S(1)}, f32[4,64,256]{2,1,0:T(8,128)}, u32[]{:S(2)}) copy-start(f32[4,64,256]{2,1,0:T(8,128)} %param.5) | copy-start | bytes 786436
  31.9 9.3 %collective-permute-start = (f32[4,8,256]{2,1,0:T(8,128)S(1)}, f32[4,8,256]{2,1,0:T(8,128)S(1)}, u32[]{:S(2)}, u32[]{:S(2)}) collective-permute-start(f32[4,8,256]{2,1,0:T(8,128)S(1)} %pad_maximum_fusion.1), channel_id=1, source_target_pairs={{0,1},{1,2},{2,3},{3,4},{4,5},{5,6},{6,7},{7,0},{8,9},{9,10},{10,1... | collective-permute-start | bytes 98312 | tf_op jit(solution)/shard_map/ppermute | solution.py:273
  35.0 6.1 %collective-permute-start.1 = (f32[4,8,256]{2,1,0:T(8,128)S(1)}, f32[4,8,256]{2,1,0:T(8,128)S(1)}, u32[]{:S(2)}, u32[]{:S(2)}) collective-permute-start(f32[4,8,256]{2,1,0:T(8,128)S(1)} %pad_maximum_fusion.2), channel_id=1, source_target_pairs={{1,0},{2,1},{3,2},{4,3},{5,4},{6,5},{7,6},{0,7},{9,8},{10,9},{11,1... | collective-permute-start | bytes 98312 | tf_op jit(solution)/shard_map/ppermute | solution.py:274
  42.7 5.2 %copy-start = (s32[768,2]{0,1:T(2,128)S(1)}, s32[768,2]{0,1:T(2,128)}, u32[]{:S(2)}) copy-start(s32[768,2]{0,1:T(2,128)} %param.8) | copy-start | bytes 18436
  42.7 5.2 %copy-start.1 = (s32[768,2]{0,1:T(2,128)S(1)}, s32[768,2]{0,1:T(2,128)}, u32[]{:S(2)}) copy-start(s32[768,2]{0,1:T(2,128)} %param.9) | copy-start | bytes 18436
  42.7 18.0 %all-to-all-start.1 = ((f16[64,4,256]{2,1,0:T(4,128)(2,1)}), f16[64,4,256]{2,1,0:T(4,128)(2,1)S(1)}, u32[]{:S(2)}, u32[]{:S(2)}) async-start(f16[64,4,256]{2,1,0:T(4,128)(2,1)} %pad_maximum_fusion), calls=%async_computation.1 | async-start | bytes 262144 | tf_op jit(solution)/shard_map/all_to_all | solution.py:283

commit v7 on v6

--- a/solution.py
+++ b/solution.py
@@ -218,29 +218,38 @@
 
     def picked(cells):
         high, low = two_terms(cells)
+
+        def one(at):
+            return matmul(high, pick_ref[:, at : at + chunk]) + matmul(low, pick_ref[:, at : at + chunk])
+
         return [
-            matmul(high, pick_ref[:, at : at + chunk]) + matmul(low, pick_ref[:, at : at + chunk])
-            for at in range(0, 2 * count, chunk)
+            rate_ref[:, at : at + chunk] * (one(at) * one(count + at))
+            for at in range(0, count, chunk)
         ]
 
-    def reacted(cells, found):
+    def reacted(cells, rates, owed, section):
         change = jnp.zeros_like(cells)
+        rest = []
         for i, at in enumerate(range(0, count, chunk)):
-            here = slice(at, at + chunk)
-            pair = found[i] * found[i + count // chunk]
-            rate_high, rate_low = two_terms(rate_ref[:, here] * pair)
-            change = change + matmul(rate_high, net_ref[here]) + matmul(rate_low, net_ref[here])
-        return cells + CHEM_STEP * change
+            rate = rates[i] + owed[i] if section else rates[i]
+            high = rate.astype(jnp.bfloat16)
+            rest.append(rate - high.astype(jnp.float32))
+            net = net_ref[at : at + chunk]
+            change = change + matmul(high, net)
+            if section == SECTIONS - 1:
+                change = change + matmul(rest[i].astype(jnp.bfloat16), net)
+        return cells + CHEM_STEP * change, rest
 
     size = cells.shape[0] // 2
     early, late = cells[:size], cells[size:]
-    found_late = picked(late)
+    owed_early = owed_late = None
+    rates_late = picked(late)
     for section in range(SECTIONS):
-        found_early = picked(early)
-        late = reacted(late, found_late)
-        early = reacted(early, found_early)
+        rates_early = picked(early)
+        late, owed_late = reacted(late, rates_late, owed_late, section)
+        early, owed_early = reacted(early, rates_early, owed_early, section)
         if section < SECTIONS - 1:
-            found_late = picked(late)
+            rates_late = picked(late)
     out_ref[...] = jnp.concatenate([early, late], 0).T.reshape(out_ref.shape)
 
 

time: 67.3 us -> 66.7 us (level)
  no operation moved by 1% of the time
where the time goes in v7:
time: 66.7 us; the launch traced here: 65.8 us
  starting transfers between devices  30.2 us (45%)
  waiting for transfers between devices  24 us (36%)
  Pallas kernels  8.1 us (12%)
  local copies, waits for them, and re-layouts  2.52 us (4%)
  other arithmetic  0.9 us (1%)
    all_to_all x1, starting transfers between devices, on_device(): lax.all_to_all(jnp.broadcast_to(wind_speeds[None], (wide, *wind_speeds.sh...  17.6 us
    all_to_all x1, waiting for transfers between devices, on_device(): cells = lax.all_to_all(moved.astype(SENT), 'wide', 0, 0, tiled=True)  12.4 us
    all_to_all x1, waiting for transfers between devices, on_device(): lax.all_to_all(jnp.broadcast_to(wind_speeds[None], (wide, *wind_speeds.sh...  11.6 us
    all_to_all x1, starting transfers between devices, on_device(): cells = lax.all_to_all(moved.astype(SENT), 'wide', 0, 0, tiled=True)  5.15 us
    pallas_call x1, Pallas kernels, chemistry(): pl.pallas_call(chemistry_kernel, out_shape=jax.ShapeDtypeStruct((S, 1, co...  5.08 us
    ppermute x1, starting transfers between devices, on_device(): lax.ppermute(rim(slice(RIM)), 'narrow', [(j, i) for i, j in down])  4.27 us
    ppermute x1, starting transfers between devices, on_device(): from_above = lax.ppermute(rim(slice(-RIM, None)), 'narrow', down)  3.12 us
    pallas_call x2, Pallas kernels, sweep_call(): pl.pallas_call(kernel, out_shape=jax.ShapeDtypeStruct((2 * (count - 2 * R...  2.46 us
  transfers between devices with their start and end apart: 4, of which 2 were waited for; matrix products, arithmetic and copies ran while one was open for 0% of the time, Pallas kernels for 3%

profile of v7, /device:TPU:1, one launch (start us, length us, event | category | flops | bytes accessed | tf_op | source)
XLA Modules:
  0.0 65.8 jit_solution(14083009192633660410)
XLA Ops:
  0.0 1.4 %broadcast_in_dim.9 = bf16[64,2,2,1,256]{4,2,1,3,0:T(2,128)(2,1)} broadcast(bf16[2,2,256]{2,1,0:T(2,128)(2,1)} %bitcast.17), dimensions={1,2,4} | broadcast | bytes 133120 | tf_op jit(solution)/shard_map/broadcast_in_dim | solution.py:273
  1.4 17.6 %all-to-all-start = ((bf16[64,2,2,1,256]{4,2,1,3,0:T(2,128)(2,1)}), bf16[64,2,2,1,256]{4,2,1,3,0:T(2,128)(2,1)S(1)}, u32[]{:S(2)}, u32[]{:S(2)}) async-start(bf16[64,2,2,1,256]{4,2,1,3,0:T(2,128)(2,1)} %broadcast_in_dim.9), calls=%async_computation | async-start | bytes 262144 | tf_op jit(solution)/shard_map/all_to_all | solution.py:272
  19.0 0.0 copy-start.3
  19.0 0.0 copy-start.2
  19.1 0.2 maps.1
  19.2 0.5 copy-done.3
  19.7 0.3 copy-done.2
  20.0 0.2 copy.9
  20.2 11.6 %all-to-all-done = bf16[64,2,2,1,256]{4,2,1,3,0:T(2,128)(2,1)S(1)} async-done(((bf16[64,2,2,1,256]{4,2,1,3,0:T(2,128)(2,1)}), bf16[64,2,2,1,256]{4,2,1,3,0:T(2,128)(2,1)S(1)}, u32[]{:S(2)}, u32[]{:S(2)}) %all-to-all-start) | async-done | bytes 131104 | tf_op jit(solution)/shard_map/all_to_all | solution.py:272
  31.9 3.1 %collective-permute-start = (f32[4,8,256]{2,1,0:T(8,128)S(1)}, f32[4,8,256]{2,1,0:T(8,128)S(1)}, u32[]{:S(2)}, u32[]{:S(2)}) collective-permute-start(f32[4,8,256]{2,1,0:T(8,128)S(1)} %pad_maximum_fusion.1), channel_id=1, source_target_pairs={{0,1},{1,2},{2,3},{3,4},{4,5},{5,6},{6,7},{7,0},{8,9},{9,10},{10,1... | collective-permute-start | bytes 98312 | tf_op jit(solution)/shard_map/ppermute | solution.py:282
  35.0 4.3 %collective-permute-start.1 = (f32[4,8,256]{2,1,0:T(8,128)S(1)}, f32[4,8,256]{2,1,0:T(8,128)S(1)}, u32[]{:S(2)}, u32[]{:S(2)}) collective-permute-start(f32[4,8,256]{2,1,0:T(8,128)S(1)} %pad_maximum_fusion.2), channel_id=1, source_target_pairs={{1,0},{2,1},{3,2},{4,3},{5,4},{6,5},{7,6},{0,7},{9,8},{10,9},{11,1... | collective-permute-start | bytes 98312 | tf_op jit(solution)/shard_map/ppermute | solution.py:283
  39.3 0.1 reshape.15.winds_ref
  39.4 1.7 %shard_map.56 = f32[56,4,256]{2,1,0:T(4,128)S(1)} custom-call(f32[64,4,256]{2,1,0:T(4,128)S(1)} %bitcast.13, bf16[64,4,256]{2,1,0:T(4,128)(2,1)S(1)} %reshape.15.winds_ref, bf16[256,1024]{1,0:T(8,128)(2,1)S(1)} %get-tuple-element.9.shift_ref, bf16[256,512]{1,0:T(8,128)(2,1)S(1)} %get-tuple-element.10.face_ref), custom_call_target="tpu_custom_call" | custom-call | flops 4000000000 | bytes 600000 | tf_op jit(solution)/shard_map/pallas_call | solution.py:167
  41.1 0.0 collective-permute-done.above_ref
  41.1 0.0 collective-permute-done.1.below_ref
  41.1 0.8 %shard_map.55 = f32[8,4,256]{2,1,0:T(4,128)S(1)} custom-call(f32[64,4,256]{2,1,0:T(4,128)S(1)} %bitcast.14, bf16[64,4,256]{2,1,0:T(4,128)(2,1)S(1)} %reshape.15.winds_ref, f32[4,8,256]{2,1,0:T(8,128)S(1)} %collective-permute-done.above_ref, f32[4,8,256]{2,1,0:T(8,128)S(1)} %collective-permute-done.1.below_ref, ...), custom_call_target="tpu_custom_call" | custom-call | flops 1000000000 | bytes 600000 | tf_op jit(solution)/shard_map/pallas_call | solution.py:167
  41.9 0.8 %pad_maximum_fusion = f16[64,4,256]{2,1,0:T(4,128)(2,1)} fusion(f16[4,4,256]{2,1,0:T(4,128)(2,1)S(1)} %get-tuple-element.18, f16[56,4,256]{2,1,0:T(4,128)(2,1)S(1)} %convert.12, f16[4,4,256]{2,1,0:T(4,128)(2,1)S(1)} %get-tuple-element.17), kind=kLoop, calls=%fused_computation.1 | loop fusion | flops 131072 | bytes 262144 | tf_op jit(solution)/shard_map/concatenate | solution.py:291
  42.7 0.0 copy-start
  42.7 0.0 copy-start.1
  42.7 5.2 %all-to-all-start.1 = ((f16[64,4,256]{2,1,0:T(4,128)(2,1)}), f16[64,4,256]{2,1,0:T(4,128)(2,1)S(1)}, u32[]{:S(2)}, u32[]{:S(2)}) async-start(f16[64,4,256]{2,1,0:T(4,128)(2,1)} %pad_maximum_fusion), calls=%async_computation.1 | async-start | bytes 262144 | tf_op jit(solution)/shard_map/all_to_all | solution.py:292
  47.9 0.0 copy-done
  47.9 0.0 copy-done.1
  47.9 0.4 tables.1
  48.3 12.4 %all-to-all-done.1 = f16[64,4,256]{2,1,0:T(4,128)(2,1)S(1)} async-done(((f16[64,4,256]{2,1,0:T(4,128)(2,1)}), f16[64,4,256]{2,1,0:T(4,128)(2,1)S(1)}, u32[]{:S(2)}, u32[]{:S(2)}) %all-to-all-start.1) | async-done | bytes 131104 | tf_op jit(solution)/shard_map/all_to_all | solution.py:292
  60.8 5.1 %chemistry.1 = f32[256,1,256]{2,1,0:T(1,128)} custom-call(f32[64,4,256]{2,1,0:T(4,128)S(1)} %convert_element_type.20.cells_ref, bf16[256,1536]{1,0:T(8,128)(2,1)S(1)} %get-tuple-element.11.pick_ref, bf16[768,256]{1,0:T(8,128)(2,1)S(1)} %get-tuple-element.12.net_ref, f32[1,768]{1,0:T(1,128)S(1)} %reshape.16.rate_ref), custom_call_target="tpu_custom_call" | custom-call | flops 4000000000 | bytes 2000000 | tf_op jit(solution)/shard_map/chemistry/pallas_call | solution.py:258
  (11 shorter events, 0.2 us)
Async XLA Ops:
  1.4 30.4 %all-to-all-start = ((bf16[64,2,2,1,256]{4,2,1,3,0:T(2,128)(2,1)}), bf16[64,2,2,1,256]{4,2,1,3,0:T(2,128)(2,1)S(1)}, u32[]{:S(2)}, u32[]{:S(2)}) async-start(bf16[64,2,2,1,256]{4,2,1,3,0:T(2,128)(2,1)} %broadcast_in_dim.9), calls=%async_computation | async-start | bytes 262144 | tf_op jit(solution)/shard_map/all_to_all | solution.py:272
  19.0 0.7 %copy-start.3 = (f32[768]{0:T(1024)S(1)}, f32[768]{0:T(1024)}, u32[]{:S(2)}) copy-start(f32[768]{0:T(1024)} %param.7) | copy-start | bytes 9220
  19.0 1.0 %copy-start.2 = (f32[4,64,256]{2,1,0:T(8,128)S(1)}, f32[4,64,256]{2,1,0:T(8,128)}, u32[]{:S(2)}) copy-start(f32[4,64,256]{2,1,0:T(8,128)} %param.5) | copy-start | bytes 786436
  31.9 9.3 %collective-permute-start = (f32[4,8,256]{2,1,0:T(8,128)S(1)}, f32[4,8,256]{2,1,0:T(8,128)S(1)}, u32[]{:S(2)}, u32[]{:S(2)}) collective-permute-start(f32[4,8,256]{2,1,0:T(8,128)S(1)} %pad_maximum_fusion.1), channel_id=1, source_target_pairs={{0,1},{1,2},{2,3},{3,4},{4,5},{5,6},{6,7},{7,0},{8,9},{9,10},{10,1... | collective-permute-start | bytes 98312 | tf_op jit(solution)/shard_map/ppermute | solution.py:282
  35.0 6.1 %collective-permute-start.1 = (f32[4,8,256]{2,1,0:T(8,128)S(1)}, f32[4,8,256]{2,1,0:T(8,128)S(1)}, u32[]{:S(2)}, u32[]{:S(2)}) collective-permute-start(f32[4,8,256]{2,1,0:T(8,128)S(1)} %pad_maximum_fusion.2), channel_id=1, source_target_pairs={{1,0},{2,1},{3,2},{4,3},{5,4},{6,5},{7,6},{0,7},{9,8},{10,9},{11,1... | collective-permute-start | bytes 98312 | tf_op jit(solution)/shard_map/ppermute | solution.py:283
  42.7 5.2 %copy-start = (s32[768,2]{0,1:T(2,128)S(1)}, s32[768,2]{0,1:T(2,128)}, u32[]{:S(2)}) copy-start(s32[768,2]{0,1:T(2,128)} %param.8) | copy-start | bytes 18436
  42.7 5.2 %copy-start.1 = (s32[768,2]{0,1:T(2,128)S(1)}, s32[768,2]{0,1:T(2,128)}, u32[]{:S(2)}) copy-start(s32[768,2]{0,1:T(2,128)} %param.9) | copy-start | bytes 18436
  42.7 18.0 %all-to-all-start.1 = ((f16[64,4,256]{2,1,0:T(4,128)(2,1)}), f16[64,4,256]{2,1,0:T(4,128)(2,1)S(1)}, u32[]{:S(2)}, u32[]{:S(2)}) async-start(f16[64,4,256]{2,1,0:T(4,128)(2,1)} %pad_maximum_fusion), calls=%async_computation.1 | async-start | bytes 262144 | tf_op jit(solution)/shard_map/all_to_all | solution.py:292
